TPU v7x, 64 devices: a 2x2x8 block of a 4x4x8 slice. The times are simulated.
64 devices in a mesh: dp: 4 (over x, y), cp: 16 (over z, core).
Axes of the slice: x: 2, y: 2, z: 8, core: 2. Of those that a mesh axis runs over, the one named last changes fastest.
The devices are a block of a 4x4x8 slice.
Arguments:
- x_seq: bfloat16 [4, 8192, 512], P('dp', 'cp'), parts along dimension 0
- dy_seq: float32 [4, 8192, 512], P('dp', 'cp'), parts along dimension 0
- ln1_gain: float32 [512], replicated
- ln1_bias: float32 [512], replicated
- ln2_gain: float32 [512], replicated
- ln2_bias: float32 [512], replicated
- w_qkv: bfloat16 [512, 8, 3, 64], replicated
- b_qkv: bfloat16 [8, 3, 64], replicated
- w_out: bfloat16 [512, 512], replicated
- b_out: bfloat16 [512], replicated
- w_up: bfloat16 [512, 2048], replicated
- b_up: bfloat16 [2048], replicated
- w_down: bfloat16 [2048, 512], replicated
- b_down: bfloat16 [512], replicated
Outputs:
- output 1: bfloat16 [4, 8192, 512], P('dp', 'cp'), parts along dimension 0
- output 2: float32 [4, 8192, 512], P('dp', 'cp'), parts along dimension 0
- output 3: float32 [2048], P('dp'), parts along dimension 0
- output 4: float32 [2048], P('dp'), parts along dimension 0
- output 5: float32 [2048], P('dp'), parts along dimension 0
- output 6: float32 [2048], P('dp'), parts along dimension 0
- output 7: float32 [2048, 8, 3, 64], P('dp'), parts along dimension 0
- output 8: float32 [32, 3, 64], P('dp'), parts along dimension 0
- output 9: float32 [2048, 512], P('dp'), parts along dimension 0
- output 10: float32 [2048], P('dp'), parts along dimension 0
- output 11: float32 [2048, 2048], P('dp'), parts along dimension 0
- output 12: float32 [8192], P('dp'), parts along dimension 0
- output 13: float32 [8192, 512], P('dp'), parts along dimension 0
- output 14: float32 [2048], P('dp'), parts along dimension 0
There are 4 independent parts. A program takes and returns all parts, laid end to end along the dimension named above; an argument that names none is the same for every part.
All inputs are finite; a program needn't handle non-finite values.
Results may differ from a plain program's by a relative error of at most 0.0196811.
Values are sent between devices in bfloat16 or wider.
A program may use at most 768 MiB of HBM per device.

v0:
```python
import jax
import jax.numpy as jnp
from jax import lax
from jax.sharding import PartitionSpec as P

EPS = 1e-5
ROPE_BASE = 10000.0
NEG_BIG = -1e30


def layer_norm(row_vals, norm_gain, norm_shift):
    row_mean = jnp.mean(row_vals, axis=-1, keepdims=True)
    centered = row_vals - row_mean
    inv_std = lax.rsqrt(jnp.mean(centered * centered, axis=-1, keepdims=True) + EPS)
    x_norm = centered * inv_std
    return x_norm * norm_gain + norm_shift, x_norm, inv_std


def norm_backward(d_out, x_norm, inv_std, norm_gain):
    d_norm = d_out * norm_gain
    d_rows = inv_std * (d_norm - jnp.mean(d_norm, axis=-1, keepdims=True) - x_norm * jnp.mean(d_norm * x_norm, axis=-1, keepdims=True))
    return d_rows, jnp.sum(d_out * x_norm, axis=(0, 1)), jnp.sum(d_out, axis=(0, 1))


def rope_tables(positions, head_dim):
    rot_dim = head_dim // 4
    inv_freq = ROPE_BASE ** (-2.0 * jnp.arange(rot_dim // 2, dtype=jnp.float32) / rot_dim)
    angles = positions.astype(jnp.float32)[:, None] * inv_freq[None, :]
    return jnp.cos(angles), jnp.sin(angles)


def apply_rotary(head_vals, cos_t, sin_t):
    half_rot = cos_t.shape[-1]
    first_half = head_vals[..., :half_rot]
    second_half = head_vals[..., half_rot:2 * half_rot]
    cos_b = cos_t[None, :, None, :]
    sin_b = sin_t[None, :, None, :]
    return jnp.concatenate([first_half * cos_b - second_half * sin_b, second_half * cos_b + first_half * sin_b, head_vals[..., 2 * half_rot:]], axis=-1)


def exact_gelu(pre_act):
    return jax.nn.gelu(pre_act, approximate=False)


def block_scores(q_rows, k_blk, qk_scale, diag_mask):
    scores = jnp.einsum('bqhe,bkhe->bhqk', q_rows, k_blk, preferred_element_type=jnp.float32) * qk_scale
    if diag_mask is None:
        return scores
    return jnp.where(diag_mask, scores, NEG_BIG)


def fold_block(soft_state, q_rows, k_blk, v_blk, qk_scale, diag_mask):
    row_max, row_sum, out_acc = soft_state
    scores = block_scores(q_rows, k_blk, qk_scale, diag_mask)
    new_max = jnp.maximum(row_max, jnp.max(scores, axis=-1))
    attn_probs = jnp.exp(scores - new_max[..., None])
    rescale = jnp.exp(row_max - new_max)
    row_sum = row_sum * rescale + jnp.sum(attn_probs, axis=-1)
    part_out = jnp.einsum('bhqk,bkhe->bqhe', attn_probs.astype(jnp.bfloat16), v_blk, preferred_element_type=jnp.float32)
    out_acc = out_acc * jnp.swapaxes(rescale, 1, 2)[..., None] + part_out
    return new_max, row_sum, out_acc


def block_grads(q_rows, k_blk, v_blk, d_ctx_bf, log_sum, row_delta, qk_scale, diag_mask):
    scores = block_scores(q_rows, k_blk, qk_scale, diag_mask)
    attn_probs = jnp.exp(scores - log_sum[..., None])
    d_v = jnp.einsum('bhqk,bqhe->bkhe', attn_probs.astype(jnp.bfloat16), d_ctx_bf, preferred_element_type=jnp.float32)
    d_probs = jnp.einsum('bqhe,bkhe->bhqk', d_ctx_bf, v_blk, preferred_element_type=jnp.float32)
    d_scores = (attn_probs * (d_probs - row_delta[..., None]) * qk_scale).astype(jnp.bfloat16)
    d_q = jnp.einsum('bhqk,bkhe->bqhe', d_scores, k_blk, preferred_element_type=jnp.float32)
    d_k = jnp.einsum('bhqk,bqhe->bkhe', d_scores, q_rows, preferred_element_type=jnp.float32)
    return d_q, d_k, d_v


def solution(mesh):
    cp_size = mesh.shape['cp']
    shift_perm = [(sender, (sender + 1) % cp_size) for sender in range(cp_size)]
    row_spec = P('dp', 'cp', None)
    in_specs = (row_spec, row_spec) + (P(),) * 12
    out_specs = (row_spec, row_spec, P('dp'), P('dp'), P('dp'), P('dp'), P('dp', None, None, None), P('dp', None, None), P('dp', None), P('dp'), P('dp', None), P('dp'), P('dp', None), P('dp'))

    def local_layer(x_blk, dy_blk, ln1_gain, ln1_bias, ln2_gain, ln2_bias, w_qkv, b_qkv, w_out, b_out, w_up, b_up, w_down, b_down):
        batch_size, row_count, model_width = x_blk.shape
        head_count, head_dim = w_qkv.shape[1], w_qkv.shape[3]
        qk_scale = head_dim ** -0.5
        my_idx = lax.axis_index('cp')
        cos_t, sin_t = rope_tables(my_idx * row_count + jnp.arange(row_count), head_dim)
        local_pos = jnp.arange(row_count)
        diag_mask = local_pos[None, :] <= local_pos[:, None]

        x_rows = x_blk.astype(jnp.float32)
        h_attn, x_norm1, inv_std1 = layer_norm(x_rows, ln1_gain, ln1_bias)
        h_attn = h_attn.astype(jnp.bfloat16)
        qkv_rows = jnp.einsum('btd,dhce->bthce', h_attn, w_qkv, preferred_element_type=jnp.float32) + b_qkv.astype(jnp.float32)
        q_rows = apply_rotary(qkv_rows[:, :, :, 0], cos_t, sin_t).astype(jnp.bfloat16)
        k_own = apply_rotary(qkv_rows[:, :, :, 1], cos_t, sin_t).astype(jnp.bfloat16)
        v_own = qkv_rows[:, :, :, 2].astype(jnp.bfloat16)

        stat_shape = (batch_size, head_count, row_count)
        start_state = (jnp.full(stat_shape, NEG_BIG, jnp.float32), jnp.zeros(stat_shape, jnp.float32), jnp.zeros((batch_size, row_count, head_count, head_dim), jnp.float32))
        own_state = fold_block(start_state, q_rows, k_own, v_own, qk_scale, diag_mask)

        def fwd_step(step_idx, carry):
            k_cur, v_cur, soft_state = carry
            k_cur, v_cur = lax.ppermute((k_cur, v_cur), 'cp', shift_perm)
            soft_state = lax.cond(step_idx <= my_idx, lambda state_in: fold_block(state_in, q_rows, k_cur, v_cur, qk_scale, None), lambda state_in: state_in, soft_state)
            return k_cur, v_cur, soft_state

        row_max, row_sum, out_acc = lax.fori_loop(1, cp_size, fwd_step, (k_own, v_own, own_state))[2]
        attn_norm = out_acc / jnp.swapaxes(row_sum, 1, 2)[..., None]
        log_sum = row_max + jnp.log(row_sum)
        attn_ctx = attn_norm.astype(jnp.bfloat16).reshape(batch_size, row_count, model_width)
        attn_proj = jnp.einsum('btd,de->bte', attn_ctx, w_out, preferred_element_type=jnp.float32) + b_out.astype(jnp.float32)

        h_mlp, x_norm2, inv_std2 = layer_norm(x_rows, ln2_gain, ln2_bias)
        h_mlp = h_mlp.astype(jnp.bfloat16)
        up_proj = jnp.einsum('btd,df->btf', h_mlp, w_up, preferred_element_type=jnp.float32) + b_up.astype(jnp.float32)
        gelu_out, gelu_back = jax.vjp(exact_gelu, up_proj)
        gelu_bf = gelu_out.astype(jnp.bfloat16)
        mlp_proj = jnp.einsum('btf,fd->btd', gelu_bf, w_down, preferred_element_type=jnp.float32) + b_down.astype(jnp.float32)
        y_rows = (x_rows + attn_proj + mlp_proj).astype(jnp.bfloat16)

        dy_bf = dy_blk.astype(jnp.bfloat16)
        dy_sum = jnp.sum(dy_blk, axis=(0, 1))
        d_w_down = jnp.einsum('btf,btd->fd', gelu_bf, dy_bf, preferred_element_type=jnp.float32)
        d_gelu = jnp.einsum('btd,fd->btf', dy_bf, w_down, preferred_element_type=jnp.float32)
        d_up = gelu_back(d_gelu)[0]
        d_b_up = jnp.sum(d_up, axis=(0, 1))
        d_up_bf = d_up.astype(jnp.bfloat16)
        d_w_up = jnp.einsum('btd,btf->df', h_mlp, d_up_bf, preferred_element_type=jnp.float32)
        d_h_mlp = jnp.einsum('btf,df->btd', d_up_bf, w_up, preferred_element_type=jnp.float32)

        d_w_out = jnp.einsum('btd,bte->de', attn_ctx, dy_bf, preferred_element_type=jnp.float32)
        d_ctx = jnp.einsum('bte,de->btd', dy_bf, w_out, preferred_element_type=jnp.float32).reshape(batch_size, row_count, head_count, head_dim)
        row_delta = jnp.swapaxes(jnp.sum(d_ctx * attn_norm, axis=-1), 1, 2)
        d_ctx_bf = d_ctx.astype(jnp.bfloat16)
        dq_own, dk_own, dv_own = block_grads(q_rows, k_own, v_own, d_ctx_bf, log_sum, row_delta, qk_scale, diag_mask)

        def bwd_step(step_idx, carry):
            k_cur, v_cur, dk_cur, dv_cur, dq_acc = carry
            k_cur, v_cur, dk_cur, dv_cur = lax.ppermute((k_cur, v_cur, dk_cur, dv_cur), 'cp', shift_perm)

            def add_block(operands):
                dq_in, dk_in, dv_in = operands
                g_q, g_k, g_v = block_grads(q_rows, k_cur, v_cur, d_ctx_bf, log_sum, row_delta, qk_scale, None)
                return dq_in + g_q, dk_in + g_k, dv_in + g_v

            dq_acc, dk_cur, dv_cur = lax.cond(step_idx <= my_idx, add_block, lambda operands: operands, (dq_acc, dk_cur, dv_cur))
            return k_cur, v_cur, dk_cur, dv_cur, dq_acc

        loop_out = lax.fori_loop(1, cp_size, bwd_step, (k_own, v_own, dk_own, dv_own, dq_own))
        d_q = loop_out[4]
        d_k, d_v = lax.ppermute((loop_out[2], loop_out[3]), 'cp', shift_perm)

        d_q_raw = apply_rotary(d_q, cos_t, -sin_t)
        d_k_raw = apply_rotary(d_k, cos_t, -sin_t)
        d_qkv = jnp.stack([d_q_raw, d_k_raw, d_v], axis=3)
        d_b_qkv = jnp.sum(d_qkv, axis=(0, 1))
        d_qkv_bf = d_qkv.astype(jnp.bfloat16)
        d_w_qkv = jnp.einsum('btd,bthce->dhce', h_attn, d_qkv_bf, preferred_element_type=jnp.float32)
        d_h_attn = jnp.einsum('bthce,dhce->btd', d_qkv_bf, w_qkv, preferred_element_type=jnp.float32)

        dx_attn, d_ln1_gain, d_ln1_bias = norm_backward(d_h_attn, x_norm1, inv_std1, ln1_gain)
        dx_mlp, d_ln2_gain, d_ln2_bias = norm_backward(d_h_mlp, x_norm2, inv_std2, ln2_gain)
        dx_rows = dy_blk + dx_attn + dx_mlp

        summed = lax.psum((d_ln1_gain, d_ln1_bias, d_ln2_gain, d_ln2_bias, d_w_qkv, d_b_qkv, d_w_out, dy_sum, d_w_up, d_b_up, d_w_down), 'cp')
        return (y_rows, dx_rows) + tuple(summed) + (summed[7],)

    return jax.shard_map(local_layer, mesh=mesh, in_specs=in_specs, out_specs=out_specs, check_vma=False)
```

profile of v0, /device:TPU:21, one launch (start us, length us, event | category | flops | bytes accessed | tf_op | source)
XLA Modules:
  0.0 1455.5 jit_solution(12512151372907441663)
XLA Ops:
  40.1 330.4 %while.42 = (s32[]{:T(128)}, bf16[1,512,8,64]{1,3,2,0:T(8,128)(2,1)}, bf16[1,512,8,64]{1,3,2,0:T(8,128)(2,1)}, f32[1,8,512]{2,1,0:T(8,128)S(1)}, f32[1,8,512]{2,...) while((s32[]{:T(128)}, ...), condition=%wide.region_9.10_spmd, body=%wide.region_4.9_spmd.sunk | while | flops 554184704 | bytes 43909520 | solution.py:109
  81.9 9.7 collective-permute-start.1
  146.3 10.2 collective-permute-start
  203.1 14.1 collective-permute-start
  228.4 14.1 collective-permute-start
  260.6 10.0 collective-permute-done.1
  274.0 11.9 collective-permute-start
  304.0 14.8 %collective-permute-done.1 = bf16[1,512,8,64]{1,3,2,0:T(8,128)(2,1)} collective-permute-done((bf16[1,512,8,64]{1,3,2,0:T(8,128)(2,1)}, bf16[1,512,8,64]{1,3,2,0:T(8,128)(2,1)}, u32[]{:S(2)}, u32[]{:S(2)}) %collective-permute-start.1) | collective-permute-done | bytes 524320 | tf_op jit(solution)/shard_map/while/body/eval_jaxpr/ppermute | solution.py:105
  322.3 20.6 %collective-permute-done.1 = bf16[1,512,8,64]{1,3,2,0:T(8,128)(2,1)} collective-permute-done((bf16[1,512,8,64]{1,3,2,0:T(8,128)(2,1)}, bf16[1,512,8,64]{1,3,2,0:T(8,128)(2,1)}, u32[]{:S(2)}, u32[]{:S(2)}) %collective-permute-start.1) | collective-permute-done | bytes 524320 | tf_op jit(solution)/shard_map/while/body/eval_jaxpr/ppermute | solution.py:105
  346.4 20.6 %collective-permute-done.1 = bf16[1,512,8,64]{1,3,2,0:T(8,128)(2,1)} collective-permute-done((bf16[1,512,8,64]{1,3,2,0:T(8,128)(2,1)}, bf16[1,512,8,64]{1,3,2,0:T(8,128)(2,1)}, u32[]{:S(2)}, u32[]{:S(2)}) %collective-permute-start.1) | collective-permute-done | bytes 524320 | tf_op jit(solution)/shard_map/while/body/eval_jaxpr/ppermute | solution.py:105
  388.0 793.0 %while.43 = (s32[]{:T(128)}, bf16[1,512,8,64]{1,3,2,0:T(8,128)(2,1)}, bf16[1,512,8,64]{1,3,2,0:T(8,128)(2,1)}, f32[1,512,8,64]{1,3,2,0:T(8,128)}, f32[1,512,8,64...) while((s32[]{:T(128)}, ...), condition=%wide.region_14.15_spmd, body=%wide.region_11.14_spmd.sunk | while | flops 1361838080 | bytes 77185552 | solution.py:151
  388.5 28.3 %collective-permute-done.3 = bf16[1,512,8,64]{1,3,2,0:T(8,128)(2,1)} collective-permute-done((bf16[1,512,8,64]{1,3,2,0:T(8,128)(2,1)}, bf16[1,512,8,64]{1,3,2,0:T(8,128)(2,1)}, u32[]{:S(2)}, u32[]{:S(2)}) %collective-permute-start.3) | collective-permute-done | bytes 524320 | tf_op jit(solution)/shard_map/while/body/eval_jaxpr/ppermute | solution.py:141
  423.3 14.8 %conditional.5 = ((f32[1,512,8,64]{1,3,2,0:T(8,128)}, f32[1,512,8,64]{1,3,2,0:T(8,128)}, f32[1,512,8,64]{1,3,2,0:T(8,128)})) conditional(s32[]{:T(128)} %convert_element_type.295, (f32[1,512,8,64]{1,3,2,0:T(8,128)}, f32[1,512,8,64]{1,3,2,0:T(8,128)}, f32[1,512,8,64]{1,3,2,0:T(8,128)}) %tuple.108, (bf16[1,512,8,64]{1,3,2,0:T(8,128)(2,1)S(1)}, ...), branch_computations={%region_12.12_spmd, %region_13.13_spmd} | conditional | flops 1361838080 | bytes 58310800 | solution.py:148
  445.2 28.5 %collective-permute-done.3 = bf16[1,512,8,64]{1,3,2,0:T(8,128)(2,1)} collective-permute-done((bf16[1,512,8,64]{1,3,2,0:T(8,128)(2,1)}, bf16[1,512,8,64]{1,3,2,0:T(8,128)(2,1)}, u32[]{:S(2)}, u32[]{:S(2)}) %collective-permute-start.3) | collective-permute-done | bytes 524320 | tf_op jit(solution)/shard_map/while/body/eval_jaxpr/ppermute | solution.py:141
  484.6 17.3 %collective-permute-start.5 = (f32[1,512,8,64]{1,3,2,0:T(8,128)}, f32[1,512,8,64]{1,3,2,0:T(8,128)}, u32[]{:S(2)}, u32[]{:S(2)}) collective-permute-start(f32[1,512,8,64]{1,3,2,0:T(8,128)} %get-tuple-element.709), channel_id=1, source_target_pairs={{0,1},{1,2},{2,3},{3,4},{4,5},{5,6},{6,7},{7,8},{8,9},{9,10},{10,1... | collective-permute-start | bytes 3145736 | tf_op jit(solution)/shard_map/while/body/eval_jaxpr/ppermute | solution.py:141
  502.0 28.5 %collective-permute-done.3 = bf16[1,512,8,64]{1,3,2,0:T(8,128)(2,1)} collective-permute-done((bf16[1,512,8,64]{1,3,2,0:T(8,128)(2,1)}, bf16[1,512,8,64]{1,3,2,0:T(8,128)(2,1)}, u32[]{:S(2)}, u32[]{:S(2)}) %collective-permute-start.3) | collective-permute-done | bytes 524320 | tf_op jit(solution)/shard_map/while/body/eval_jaxpr/ppermute | solution.py:141
  555.8 16.7 %collective-permute-done.3 = bf16[1,512,8,64]{1,3,2,0:T(8,128)(2,1)} collective-permute-done((bf16[1,512,8,64]{1,3,2,0:T(8,128)(2,1)}, bf16[1,512,8,64]{1,3,2,0:T(8,128)(2,1)}, u32[]{:S(2)}, u32[]{:S(2)}) %collective-permute-start.3) | collective-permute-done | bytes 524320 | tf_op jit(solution)/shard_map/while/body/eval_jaxpr/ppermute | solution.py:141
  588.5 17.3 %collective-permute-start.3 = (bf16[1,512,8,64]{1,3,2,0:T(8,128)(2,1)}, bf16[1,512,8,64]{1,3,2,0:T(8,128)(2,1)}, u32[]{:S(2)}, u32[]{:S(2)}) collective-permute-start(bf16[1,512,8,64]{1,3,2,0:T(8,128)(2,1)} %get-tuple-element.707), channel_id=1, source_target_pairs={{0,1},{1,2},{2,3},{3,4},{4,5},{5,6},{6,7},{7,8},{8,9},{9,10},{10,1... | collective-permute-start | bytes 1572872 | tf_op jit(solution)/shard_map/while/body/eval_jaxpr/ppermute | solution.py:141
  612.6 11.5 collective-permute-done.3
  631.3 14.0 collective-permute-start.4
  647.8 22.1 %collective-permute-start.2 = (bf16[1,512,8,64]{1,3,2,0:T(8,128)(2,1)}, bf16[1,512,8,64]{1,3,2,0:T(8,128)(2,1)S(1)}, u32[]{:S(2)}, u32[]{:S(2)}) collective-permute-start(bf16[1,512,8,64]{1,3,2,0:T(8,128)(2,1)} %get-tuple-element.706), channel_id=1, source_target_pairs={{0,1},{1,2},{2,3},{3,4},{4,5},{5,6},{6,7},{7,8},{8,9},{9,10},{10,1... | collective-permute-start | bytes 1572872 | tf_op jit(solution)/shard_map/while/body/eval_jaxpr/ppermute | solution.py:141
  685.6 12.5 collective-permute-start.4
  700.6 12.4 collective-permute-start.2
  713.0 19.6 %collective-permute-done.3 = bf16[1,512,8,64]{1,3,2,0:T(8,128)(2,1)} collective-permute-done((bf16[1,512,8,64]{1,3,2,0:T(8,128)(2,1)}, bf16[1,512,8,64]{1,3,2,0:T(8,128)(2,1)}, u32[]{:S(2)}, u32[]{:S(2)}) %collective-permute-start.3) | collective-permute-done | bytes 524320 | tf_op jit(solution)/shard_map/while/body/eval_jaxpr/ppermute | solution.py:141
  739.9 14.3 collective-permute-start.4
  756.7 14.4 collective-permute-start.2
  771.0 15.9 %collective-permute-done.3 = bf16[1,512,8,64]{1,3,2,0:T(8,128)(2,1)} collective-permute-done((bf16[1,512,8,64]{1,3,2,0:T(8,128)(2,1)}, bf16[1,512,8,64]{1,3,2,0:T(8,128)(2,1)}, u32[]{:S(2)}, u32[]{:S(2)}) %collective-permute-start.3) | collective-permute-done | bytes 524320 | tf_op jit(solution)/shard_map/while/body/eval_jaxpr/ppermute | solution.py:141
  794.2 18.0 %collective-permute-start.4 = (f32[1,512,8,64]{1,3,2,0:T(8,128)}, f32[1,512,8,64]{1,3,2,0:T(8,128)}, u32[]{:S(2)}, u32[]{:S(2)}) collective-permute-start(f32[1,512,8,64]{1,3,2,0:T(8,128)} %get-tuple-element.708), channel_id=1, source_target_pairs={{0,1},{1,2},{2,3},{3,4},{4,5},{5,6},{6,7},{7,8},{8,9},{9,10},{10,1... | collective-permute-start | bytes 3145736 | tf_op jit(solution)/shard_map/while/body/eval_jaxpr/ppermute | solution.py:141
  814.7 14.4 collective-permute-start.2
  829.0 12.2 collective-permute-done.3
  848.5 8.8 collective-permute-start.4
  857.3 12.4 collective-permute-start.3
  869.7 9.8 collective-permute-start.2
  879.5 16.1 %collective-permute-done.3 = bf16[1,512,8,64]{1,3,2,0:T(8,128)(2,1)} collective-permute-done((bf16[1,512,8,64]{1,3,2,0:T(8,128)(2,1)}, bf16[1,512,8,64]{1,3,2,0:T(8,128)(2,1)}, u32[]{:S(2)}, u32[]{:S(2)}) %collective-permute-start.3) | collective-permute-done | bytes 524320 | tf_op jit(solution)/shard_map/while/body/eval_jaxpr/ppermute | solution.py:141
  902.8 10.6 collective-permute-start.4
  915.9 14.4 collective-permute-start.2
  930.3 19.6 %collective-permute-done.3 = bf16[1,512,8,64]{1,3,2,0:T(8,128)(2,1)} collective-permute-done((bf16[1,512,8,64]{1,3,2,0:T(8,128)(2,1)}, bf16[1,512,8,64]{1,3,2,0:T(8,128)(2,1)}, u32[]{:S(2)}, u32[]{:S(2)}) %collective-permute-start.3) | collective-permute-done | bytes 524320 | tf_op jit(solution)/shard_map/while/body/eval_jaxpr/ppermute | solution.py:141
  961.0 12.4 collective-permute-start.2
  973.5 30.7 %collective-permute-done.3 = bf16[1,512,8,64]{1,3,2,0:T(8,128)(2,1)} collective-permute-done((bf16[1,512,8,64]{1,3,2,0:T(8,128)(2,1)}, bf16[1,512,8,64]{1,3,2,0:T(8,128)(2,1)}, u32[]{:S(2)}, u32[]{:S(2)}) %collective-permute-start.3) | collective-permute-done | bytes 524320 | tf_op jit(solution)/shard_map/while/body/eval_jaxpr/ppermute | solution.py:141
  1011.4 11.6 collective-permute-start.2
  1023.1 37.2 %collective-permute-done.3 = bf16[1,512,8,64]{1,3,2,0:T(8,128)(2,1)} collective-permute-done((bf16[1,512,8,64]{1,3,2,0:T(8,128)(2,1)}, bf16[1,512,8,64]{1,3,2,0:T(8,128)(2,1)}, u32[]{:S(2)}, u32[]{:S(2)}) %collective-permute-start.3) | collective-permute-done | bytes 524320 | tf_op jit(solution)/shard_map/while/body/eval_jaxpr/ppermute | solution.py:141
  1067.5 9.4 collective-permute-start.2
  1076.9 40.2 %collective-permute-done.3 = bf16[1,512,8,64]{1,3,2,0:T(8,128)(2,1)} collective-permute-done((bf16[1,512,8,64]{1,3,2,0:T(8,128)(2,1)}, bf16[1,512,8,64]{1,3,2,0:T(8,128)(2,1)}, u32[]{:S(2)}, u32[]{:S(2)}) %collective-permute-start.3) | collective-permute-done | bytes 524320 | tf_op jit(solution)/shard_map/while/body/eval_jaxpr/ppermute | solution.py:141
  1129.5 44.3 %collective-permute-done.3 = bf16[1,512,8,64]{1,3,2,0:T(8,128)(2,1)} collective-permute-done((bf16[1,512,8,64]{1,3,2,0:T(8,128)(2,1)}, bf16[1,512,8,64]{1,3,2,0:T(8,128)(2,1)}, u32[]{:S(2)}, u32[]{:S(2)}) %collective-permute-start.3) | collective-permute-done | bytes 524320 | tf_op jit(solution)/shard_map/while/body/eval_jaxpr/ppermute | solution.py:141
  1182.4 11.3 multiply_convert_fusion.2
  1205.4 23.1 %collective-permute-done.6 = f32[1,512,8,64]{1,3,2,0:T(8,128)S(1)} collective-permute-done((f32[1,512,8,64]{1,3,2,0:T(8,128)}, f32[1,512,8,64]{1,3,2,0:T(8,128)S(1)}, u32[]{:S(2)}, u32[]{:S(2)}) %collective-permute-start.6) | collective-permute-done | bytes 1048608 | tf_op jit(solution)/shard_map/ppermute | solution.py:153
  1248.0 95.3 %all-reduce = (f32[512]{0:T(512)}, f32[512]{0:T(512)}, f32[512]{0:T(512)}, f32[512]{0:T(512)}, f32[8,3,64]{2,0,1:T(8,128)}, /*index=5*/f32[512]{0:T(512)S(1)}, f32[2048]{0:T(1024)}) all-reduce(f32[512]{0:T(512)S(1)} %get-tuple-element.431, f32[512]{0:T(512)S(1)} %get-tuple-element.428, ...), channel_id=1, replica_groups=mesh['dp'=4,'cp'=16] {'cp'}, use_global_device_ids=true, to_apply=%region_20.21 | all-reduce | flops 6144 | bytes 49152 | tf_op jit(solution)/shard_map/psum | solution.py:167
  1346.7 90.1 %all-reduce.4.cloned.1.call-done = (f32[512,8,3,64]{0,3,2,1:T(8,128)}, f32[512,512]{1,0:T(8,128)}, f32[512,2048]{1,0:T(8,128)}, f32[2048,512]{1,0:T(8,128)}) async-done(((f32[512,8,3,64]{0,3,2,1:T(8,128)}, f32[512,512]{1,0:T(8,128)}, f32[512,2048]{1,0:T(8,128)}, f32[2048,512]{1,0:T(8,128)}), (f32[512,8,3,64]{0,3,2,1:T(8,128)}, f32[512,512]{1,0:T(8,128)}, f32[512,2048]{1,0:T(8,128)}, ...) | async-done | bytes 12582928 | tf_op jit(solution)/shard_map/psum | solution.py:167
  (502 shorter events, 505.4 us)
Async XLA Ops:
  7.2 1429.6 %all-reduce.4.cloned.1.call-start = ((), (), s32[]{:S(2)}) async-start(), calls=%async_computation | async-start | bytes 25165824 | tf_op jit(solution)/shard_map/psum | solution.py:167
  388.2 35.1 %collective-permute-start.5 = (f32[1,512,8,64]{1,3,2,0:T(8,128)}, f32[1,512,8,64]{1,3,2,0:T(8,128)}, u32[]{:S(2)}, u32[]{:S(2)}) collective-permute-start(f32[1,512,8,64]{1,3,2,0:T(8,128)} %get-tuple-element.709), channel_id=1, source_target_pairs={{0,1},{1,2},{2,3},{3,4},{4,5},{5,6},{6,7},{7,8},{8,9},{9,10},{10,1... | collective-permute-start | bytes 3145736 | tf_op jit(solution)/shard_map/while/body/eval_jaxpr/ppermute | solution.py:141
  388.3 35.0 %collective-permute-start.4 = (f32[1,512,8,64]{1,3,2,0:T(8,128)}, f32[1,512,8,64]{1,3,2,0:T(8,128)}, u32[]{:S(2)}, u32[]{:S(2)}) collective-permute-start(f32[1,512,8,64]{1,3,2,0:T(8,128)} %get-tuple-element.708), channel_id=1, source_target_pairs={{0,1},{1,2},{2,3},{3,4},{4,5},{5,6},{6,7},{7,8},{8,9},{9,10},{10,1... | collective-permute-start | bytes 3145736 | tf_op jit(solution)/shard_map/while/body/eval_jaxpr/ppermute | solution.py:141
  442.6 37.5 %collective-permute-start.5 = (f32[1,512,8,64]{1,3,2,0:T(8,128)}, f32[1,512,8,64]{1,3,2,0:T(8,128)}, u32[]{:S(2)}, u32[]{:S(2)}) collective-permute-start(f32[1,512,8,64]{1,3,2,0:T(8,128)} %get-tuple-element.709), channel_id=1, source_target_pairs={{0,1},{1,2},{2,3},{3,4},{4,5},{5,6},{6,7},{7,8},{8,9},{9,10},{10,1... | collective-permute-start | bytes 3145736 | tf_op jit(solution)/shard_map/while/body/eval_jaxpr/ppermute | solution.py:141
  445.1 35.0 %collective-permute-start.4 = (f32[1,512,8,64]{1,3,2,0:T(8,128)}, f32[1,512,8,64]{1,3,2,0:T(8,128)}, u32[]{:S(2)}, u32[]{:S(2)}) collective-permute-start(f32[1,512,8,64]{1,3,2,0:T(8,128)} %get-tuple-element.708), channel_id=1, source_target_pairs={{0,1},{1,2},{2,3},{3,4},{4,5},{5,6},{6,7},{7,8},{8,9},{9,10},{10,1... | collective-permute-start | bytes 3145736 | tf_op jit(solution)/shard_map/while/body/eval_jaxpr/ppermute | solution.py:141
  445.2 34.2 %collective-permute-start.2 = (bf16[1,512,8,64]{1,3,2,0:T(8,128)(2,1)}, bf16[1,512,8,64]{1,3,2,0:T(8,128)(2,1)S(1)}, u32[]{:S(2)}, u32[]{:S(2)}) collective-permute-start(bf16[1,512,8,64]{1,3,2,0:T(8,128)(2,1)} %get-tuple-element.706), channel_id=1, source_target_pairs={{0,1},{1,2},{2,3},{3,4},{4,5},{5,6},{6,7},{7,8},{8,9},{9,10},{10,1... | collective-permute-start | bytes 1572872 | tf_op jit(solution)/shard_map/while/body/eval_jaxpr/ppermute | solution.py:141
  484.6 52.3 %collective-permute-start.5 = (f32[1,512,8,64]{1,3,2,0:T(8,128)}, f32[1,512,8,64]{1,3,2,0:T(8,128)}, u32[]{:S(2)}, u32[]{:S(2)}) collective-permute-start(f32[1,512,8,64]{1,3,2,0:T(8,128)} %get-tuple-element.709), channel_id=1, source_target_pairs={{0,1},{1,2},{2,3},{3,4},{4,5},{5,6},{6,7},{7,8},{8,9},{9,10},{10,1... | collective-permute-start | bytes 3145736 | tf_op jit(solution)/shard_map/while/body/eval_jaxpr/ppermute | solution.py:141
  501.9 35.0 %collective-permute-start.4 = (f32[1,512,8,64]{1,3,2,0:T(8,128)}, f32[1,512,8,64]{1,3,2,0:T(8,128)}, u32[]{:S(2)}, u32[]{:S(2)}) collective-permute-start(f32[1,512,8,64]{1,3,2,0:T(8,128)} %get-tuple-element.708), channel_id=1, source_target_pairs={{0,1},{1,2},{2,3},{3,4},{4,5},{5,6},{6,7},{7,8},{8,9},{9,10},{10,1... | collective-permute-start | bytes 3145736 | tf_op jit(solution)/shard_map/while/body/eval_jaxpr/ppermute | solution.py:141
  501.9 34.2 %collective-permute-start.2 = (bf16[1,512,8,64]{1,3,2,0:T(8,128)(2,1)}, bf16[1,512,8,64]{1,3,2,0:T(8,128)(2,1)S(1)}, u32[]{:S(2)}, u32[]{:S(2)}) collective-permute-start(bf16[1,512,8,64]{1,3,2,0:T(8,128)(2,1)} %get-tuple-element.706), channel_id=1, source_target_pairs={{0,1},{1,2},{2,3},{3,4},{4,5},{5,6},{6,7},{7,8},{8,9},{9,10},{10,1... | collective-permute-start | bytes 1572872 | tf_op jit(solution)/shard_map/while/body/eval_jaxpr/ppermute | solution.py:141
  541.4 37.5 %collective-permute-start.5 = (f32[1,512,8,64]{1,3,2,0:T(8,128)}, f32[1,512,8,64]{1,3,2,0:T(8,128)}, u32[]{:S(2)}, u32[]{:S(2)}) collective-permute-start(f32[1,512,8,64]{1,3,2,0:T(8,128)} %get-tuple-element.709), channel_id=1, source_target_pairs={{0,1},{1,2},{2,3},{3,4},{4,5},{5,6},{6,7},{7,8},{8,9},{9,10},{10,1... | collective-permute-start | bytes 3145736 | tf_op jit(solution)/shard_map/while/body/eval_jaxpr/ppermute | solution.py:141
  543.9 35.0 %collective-permute-start.4 = (f32[1,512,8,64]{1,3,2,0:T(8,128)}, f32[1,512,8,64]{1,3,2,0:T(8,128)}, u32[]{:S(2)}, u32[]{:S(2)}) collective-permute-start(f32[1,512,8,64]{1,3,2,0:T(8,128)} %get-tuple-element.708), channel_id=1, source_target_pairs={{0,1},{1,2},{2,3},{3,4},{4,5},{5,6},{6,7},{7,8},{8,9},{9,10},{10,1... | collective-permute-start | bytes 3145736 | tf_op jit(solution)/shard_map/while/body/eval_jaxpr/ppermute | solution.py:141
  583.4 43.4 %collective-permute-start.5 = (f32[1,512,8,64]{1,3,2,0:T(8,128)}, f32[1,512,8,64]{1,3,2,0:T(8,128)}, u32[]{:S(2)}, u32[]{:S(2)}) collective-permute-start(f32[1,512,8,64]{1,3,2,0:T(8,128)} %get-tuple-element.709), channel_id=1, source_target_pairs={{0,1},{1,2},{2,3},{3,4},{4,5},{5,6},{6,7},{7,8},{8,9},{9,10},{10,1... | collective-permute-start | bytes 3145736 | tf_op jit(solution)/shard_map/while/body/eval_jaxpr/ppermute | solution.py:141
  585.9 40.9 %collective-permute-start.4 = (f32[1,512,8,64]{1,3,2,0:T(8,128)}, f32[1,512,8,64]{1,3,2,0:T(8,128)}, u32[]{:S(2)}, u32[]{:S(2)}) collective-permute-start(f32[1,512,8,64]{1,3,2,0:T(8,128)} %get-tuple-element.708), channel_id=1, source_target_pairs={{0,1},{1,2},{2,3},{3,4},{4,5},{5,6},{6,7},{7,8},{8,9},{9,10},{10,1... | collective-permute-start | bytes 3145736 | tf_op jit(solution)/shard_map/while/body/eval_jaxpr/ppermute | solution.py:141
  588.5 35.6 %collective-permute-start.3 = (bf16[1,512,8,64]{1,3,2,0:T(8,128)(2,1)}, bf16[1,512,8,64]{1,3,2,0:T(8,128)(2,1)}, u32[]{:S(2)}, u32[]{:S(2)}) collective-permute-start(bf16[1,512,8,64]{1,3,2,0:T(8,128)(2,1)} %get-tuple-element.707), channel_id=1, source_target_pairs={{0,1},{1,2},{2,3},{3,4},{4,5},{5,6},{6,7},{7,8},{8,9},{9,10},{10,1... | collective-permute-start | bytes 1572872 | tf_op jit(solution)/shard_map/while/body/eval_jaxpr/ppermute | solution.py:141
  631.3 49.8 %collective-permute-start.5 = (f32[1,512,8,64]{1,3,2,0:T(8,128)}, f32[1,512,8,64]{1,3,2,0:T(8,128)}, u32[]{:S(2)}, u32[]{:S(2)}) collective-permute-start(f32[1,512,8,64]{1,3,2,0:T(8,128)} %get-tuple-element.709), channel_id=1, source_target_pairs={{0,1},{1,2},{2,3},{3,4},{4,5},{5,6},{6,7},{7,8},{8,9},{9,10},{10,1... | collective-permute-start | bytes 3145736 | tf_op jit(solution)/shard_map/while/body/eval_jaxpr/ppermute | solution.py:141
  631.3 49.8 %collective-permute-start.4 = (f32[1,512,8,64]{1,3,2,0:T(8,128)}, f32[1,512,8,64]{1,3,2,0:T(8,128)}, u32[]{:S(2)}, u32[]{:S(2)}) collective-permute-start(f32[1,512,8,64]{1,3,2,0:T(8,128)} %get-tuple-element.708), channel_id=1, source_target_pairs={{0,1},{1,2},{2,3},{3,4},{4,5},{5,6},{6,7},{7,8},{8,9},{9,10},{10,1... | collective-permute-start | bytes 3145736 | tf_op jit(solution)/shard_map/while/body/eval_jaxpr/ppermute | solution.py:141
  685.6 49.8 %collective-permute-start.5 = (f32[1,512,8,64]{1,3,2,0:T(8,128)}, f32[1,512,8,64]{1,3,2,0:T(8,128)}, u32[]{:S(2)}, u32[]{:S(2)}) collective-permute-start(f32[1,512,8,64]{1,3,2,0:T(8,128)} %get-tuple-element.709), channel_id=1, source_target_pairs={{0,1},{1,2},{2,3},{3,4},{4,5},{5,6},{6,7},{7,8},{8,9},{9,10},{10,1... | collective-permute-start | bytes 3145736 | tf_op jit(solution)/shard_map/while/body/eval_jaxpr/ppermute | solution.py:141
  685.6 49.8 %collective-permute-start.4 = (f32[1,512,8,64]{1,3,2,0:T(8,128)}, f32[1,512,8,64]{1,3,2,0:T(8,128)}, u32[]{:S(2)}, u32[]{:S(2)}) collective-permute-start(f32[1,512,8,64]{1,3,2,0:T(8,128)} %get-tuple-element.708), channel_id=1, source_target_pairs={{0,1},{1,2},{2,3},{3,4},{4,5},{5,6},{6,7},{7,8},{8,9},{9,10},{10,1... | collective-permute-start | bytes 3145736 | tf_op jit(solution)/shard_map/while/body/eval_jaxpr/ppermute | solution.py:141
  698.1 34.6 %collective-permute-start.3 = (bf16[1,512,8,64]{1,3,2,0:T(8,128)(2,1)}, bf16[1,512,8,64]{1,3,2,0:T(8,128)(2,1)}, u32[]{:S(2)}, u32[]{:S(2)}) collective-permute-start(bf16[1,512,8,64]{1,3,2,0:T(8,128)(2,1)} %get-tuple-element.707), channel_id=1, source_target_pairs={{0,1},{1,2},{2,3},{3,4},{4,5},{5,6},{6,7},{7,8},{8,9},{9,10},{10,1... | collective-permute-start | bytes 1572872 | tf_op jit(solution)/shard_map/while/body/eval_jaxpr/ppermute | solution.py:141
  739.9 49.8 %collective-permute-start.5 = (f32[1,512,8,64]{1,3,2,0:T(8,128)}, f32[1,512,8,64]{1,3,2,0:T(8,128)}, u32[]{:S(2)}, u32[]{:S(2)}) collective-permute-start(f32[1,512,8,64]{1,3,2,0:T(8,128)} %get-tuple-element.709), channel_id=1, source_target_pairs={{0,1},{1,2},{2,3},{3,4},{4,5},{5,6},{6,7},{7,8},{8,9},{9,10},{10,1... | collective-permute-start | bytes 3145736 | tf_op jit(solution)/shard_map/while/body/eval_jaxpr/ppermute | solution.py:141
  739.9 49.8 %collective-permute-start.4 = (f32[1,512,8,64]{1,3,2,0:T(8,128)}, f32[1,512,8,64]{1,3,2,0:T(8,128)}, u32[]{:S(2)}, u32[]{:S(2)}) collective-permute-start(f32[1,512,8,64]{1,3,2,0:T(8,128)} %get-tuple-element.708), channel_id=1, source_target_pairs={{0,1},{1,2},{2,3},{3,4},{4,5},{5,6},{6,7},{7,8},{8,9},{9,10},{10,1... | collective-permute-start | bytes 3145736 | tf_op jit(solution)/shard_map/while/body/eval_jaxpr/ppermute | solution.py:141
  794.2 49.8 %collective-permute-start.5 = (f32[1,512,8,64]{1,3,2,0:T(8,128)}, f32[1,512,8,64]{1,3,2,0:T(8,128)}, u32[]{:S(2)}, u32[]{:S(2)}) collective-permute-start(f32[1,512,8,64]{1,3,2,0:T(8,128)} %get-tuple-element.709), channel_id=1, source_target_pairs={{0,1},{1,2},{2,3},{3,4},{4,5},{5,6},{6,7},{7,8},{8,9},{9,10},{10,1... | collective-permute-start | bytes 3145736 | tf_op jit(solution)/shard_map/while/body/eval_jaxpr/ppermute | solution.py:141
  794.2 49.8 %collective-permute-start.4 = (f32[1,512,8,64]{1,3,2,0:T(8,128)}, f32[1,512,8,64]{1,3,2,0:T(8,128)}, u32[]{:S(2)}, u32[]{:S(2)}) collective-permute-start(f32[1,512,8,64]{1,3,2,0:T(8,128)} %get-tuple-element.708), channel_id=1, source_target_pairs={{0,1},{1,2},{2,3},{3,4},{4,5},{5,6},{6,7},{7,8},{8,9},{9,10},{10,1... | collective-permute-start | bytes 3145736 | tf_op jit(solution)/shard_map/while/body/eval_jaxpr/ppermute | solution.py:141
  848.5 49.8 %collective-permute-start.5 = (f32[1,512,8,64]{1,3,2,0:T(8,128)}, f32[1,512,8,64]{1,3,2,0:T(8,128)}, u32[]{:S(2)}, u32[]{:S(2)}) collective-permute-start(f32[1,512,8,64]{1,3,2,0:T(8,128)} %get-tuple-element.709), channel_id=1, source_target_pairs={{0,1},{1,2},{2,3},{3,4},{4,5},{5,6},{6,7},{7,8},{8,9},{9,10},{10,1... | collective-permute-start | bytes 3145736 | tf_op jit(solution)/shard_map/while/body/eval_jaxpr/ppermute | solution.py:141
  848.5 49.8 %collective-permute-start.4 = (f32[1,512,8,64]{1,3,2,0:T(8,128)}, f32[1,512,8,64]{1,3,2,0:T(8,128)}, u32[]{:S(2)}, u32[]{:S(2)}) collective-permute-start(f32[1,512,8,64]{1,3,2,0:T(8,128)} %get-tuple-element.708), channel_id=1, source_target_pairs={{0,1},{1,2},{2,3},{3,4},{4,5},{5,6},{6,7},{7,8},{8,9},{9,10},{10,1... | collective-permute-start | bytes 3145736 | tf_op jit(solution)/shard_map/while/body/eval_jaxpr/ppermute | solution.py:141
  857.3 38.3 %collective-permute-start.3 = (bf16[1,512,8,64]{1,3,2,0:T(8,128)(2,1)}, bf16[1,512,8,64]{1,3,2,0:T(8,128)(2,1)}, u32[]{:S(2)}, u32[]{:S(2)}) collective-permute-start(bf16[1,512,8,64]{1,3,2,0:T(8,128)(2,1)} %get-tuple-element.707), channel_id=1, source_target_pairs={{0,1},{1,2},{2,3},{3,4},{4,5},{5,6},{6,7},{7,8},{8,9},{9,10},{10,1... | collective-permute-start | bytes 1572872 | tf_op jit(solution)/shard_map/while/body/eval_jaxpr/ppermute | solution.py:141
  902.8 49.8 %collective-permute-start.5 = (f32[1,512,8,64]{1,3,2,0:T(8,128)}, f32[1,512,8,64]{1,3,2,0:T(8,128)}, u32[]{:S(2)}, u32[]{:S(2)}) collective-permute-start(f32[1,512,8,64]{1,3,2,0:T(8,128)} %get-tuple-element.709), channel_id=1, source_target_pairs={{0,1},{1,2},{2,3},{3,4},{4,5},{5,6},{6,7},{7,8},{8,9},{9,10},{10,1... | collective-permute-start | bytes 3145736 | tf_op jit(solution)/shard_map/while/body/eval_jaxpr/ppermute | solution.py:141
  902.8 49.8 %collective-permute-start.4 = (f32[1,512,8,64]{1,3,2,0:T(8,128)}, f32[1,512,8,64]{1,3,2,0:T(8,128)}, u32[]{:S(2)}, u32[]{:S(2)}) collective-permute-start(f32[1,512,8,64]{1,3,2,0:T(8,128)} %get-tuple-element.708), channel_id=1, source_target_pairs={{0,1},{1,2},{2,3},{3,4},{4,5},{5,6},{6,7},{7,8},{8,9},{9,10},{10,1... | collective-permute-start | bytes 3145736 | tf_op jit(solution)/shard_map/while/body/eval_jaxpr/ppermute | solution.py:141
  913.4 36.5 %collective-permute-start.3 = (bf16[1,512,8,64]{1,3,2,0:T(8,128)(2,1)}, bf16[1,512,8,64]{1,3,2,0:T(8,128)(2,1)}, u32[]{:S(2)}, u32[]{:S(2)}) collective-permute-start(bf16[1,512,8,64]{1,3,2,0:T(8,128)(2,1)} %get-tuple-element.707), channel_id=1, source_target_pairs={{0,1},{1,2},{2,3},{3,4},{4,5},{5,6},{6,7},{7,8},{8,9},{9,10},{10,1... | collective-permute-start | bytes 1572872 | tf_op jit(solution)/shard_map/while/body/eval_jaxpr/ppermute | solution.py:141
  915.9 35.8 %collective-permute-start.2 = (bf16[1,512,8,64]{1,3,2,0:T(8,128)(2,1)}, bf16[1,512,8,64]{1,3,2,0:T(8,128)(2,1)S(1)}, u32[]{:S(2)}, u32[]{:S(2)}) collective-permute-start(bf16[1,512,8,64]{1,3,2,0:T(8,128)(2,1)} %get-tuple-element.706), channel_id=1, source_target_pairs={{0,1},{1,2},{2,3},{3,4},{4,5},{5,6},{6,7},{7,8},{8,9},{9,10},{10,1... | collective-permute-start | bytes 1572872 | tf_op jit(solution)/shard_map/while/body/eval_jaxpr/ppermute | solution.py:141
  957.1 49.8 %collective-permute-start.5 = (f32[1,512,8,64]{1,3,2,0:T(8,128)}, f32[1,512,8,64]{1,3,2,0:T(8,128)}, u32[]{:S(2)}, u32[]{:S(2)}) collective-permute-start(f32[1,512,8,64]{1,3,2,0:T(8,128)} %get-tuple-element.709), channel_id=1, source_target_pairs={{0,1},{1,2},{2,3},{3,4},{4,5},{5,6},{6,7},{7,8},{8,9},{9,10},{10,1... | collective-permute-start | bytes 3145736 | tf_op jit(solution)/shard_map/while/body/eval_jaxpr/ppermute | solution.py:141
  957.1 49.8 %collective-permute-start.4 = (f32[1,512,8,64]{1,3,2,0:T(8,128)}, f32[1,512,8,64]{1,3,2,0:T(8,128)}, u32[]{:S(2)}, u32[]{:S(2)}) collective-permute-start(f32[1,512,8,64]{1,3,2,0:T(8,128)} %get-tuple-element.708), channel_id=1, source_target_pairs={{0,1},{1,2},{2,3},{3,4},{4,5},{5,6},{6,7},{7,8},{8,9},{9,10},{10,1... | collective-permute-start | bytes 3145736 | tf_op jit(solution)/shard_map/while/body/eval_jaxpr/ppermute | solution.py:141
  958.5 45.6 %collective-permute-start.3 = (bf16[1,512,8,64]{1,3,2,0:T(8,128)(2,1)}, bf16[1,512,8,64]{1,3,2,0:T(8,128)(2,1)}, u32[]{:S(2)}, u32[]{:S(2)}) collective-permute-start(bf16[1,512,8,64]{1,3,2,0:T(8,128)(2,1)} %get-tuple-element.707), channel_id=1, source_target_pairs={{0,1},{1,2},{2,3},{3,4},{4,5},{5,6},{6,7},{7,8},{8,9},{9,10},{10,1... | collective-permute-start | bytes 1572872 | tf_op jit(solution)/shard_map/while/body/eval_jaxpr/ppermute | solution.py:141
  961.0 45.0 %collective-permute-start.2 = (bf16[1,512,8,64]{1,3,2,0:T(8,128)(2,1)}, bf16[1,512,8,64]{1,3,2,0:T(8,128)(2,1)S(1)}, u32[]{:S(2)}, u32[]{:S(2)}) collective-permute-start(bf16[1,512,8,64]{1,3,2,0:T(8,128)(2,1)} %get-tuple-element.706), channel_id=1, source_target_pairs={{0,1},{1,2},{2,3},{3,4},{4,5},{5,6},{6,7},{7,8},{8,9},{9,10},{10,1... | collective-permute-start | bytes 1572872 | tf_op jit(solution)/shard_map/while/body/eval_jaxpr/ppermute | solution.py:141
  1011.4 51.6 %collective-permute-start.5 = (f32[1,512,8,64]{1,3,2,0:T(8,128)}, f32[1,512,8,64]{1,3,2,0:T(8,128)}, u32[]{:S(2)}, u32[]{:S(2)}) collective-permute-start(f32[1,512,8,64]{1,3,2,0:T(8,128)} %get-tuple-element.709), channel_id=1, source_target_pairs={{0,1},{1,2},{2,3},{3,4},{4,5},{5,6},{6,7},{7,8},{8,9},{9,10},{10,1... | collective-permute-start | bytes 3145736 | tf_op jit(solution)/shard_map/while/body/eval_jaxpr/ppermute | solution.py:141
  1011.4 51.6 %collective-permute-start.4 = (f32[1,512,8,64]{1,3,2,0:T(8,128)}, f32[1,512,8,64]{1,3,2,0:T(8,128)}, u32[]{:S(2)}, u32[]{:S(2)}) collective-permute-start(f32[1,512,8,64]{1,3,2,0:T(8,128)} %get-tuple-element.708), channel_id=1, source_target_pairs={{0,1},{1,2},{2,3},{3,4},{4,5},{5,6},{6,7},{7,8},{8,9},{9,10},{10,1... | collective-permute-start | bytes 3145736 | tf_op jit(solution)/shard_map/while/body/eval_jaxpr/ppermute | solution.py:141
  1011.4 48.9 %collective-permute-start.3 = (bf16[1,512,8,64]{1,3,2,0:T(8,128)(2,1)}, bf16[1,512,8,64]{1,3,2,0:T(8,128)(2,1)}, u32[]{:S(2)}, u32[]{:S(2)}) collective-permute-start(bf16[1,512,8,64]{1,3,2,0:T(8,128)(2,1)} %get-tuple-element.707), channel_id=1, source_target_pairs={{0,1},{1,2},{2,3},{3,4},{4,5},{5,6},{6,7},{7,8},{8,9},{9,10},{10,1... | collective-permute-start | bytes 1572872 | tf_op jit(solution)/shard_map/while/body/eval_jaxpr/ppermute | solution.py:141
  1011.4 50.7 %collective-permute-start.2 = (bf16[1,512,8,64]{1,3,2,0:T(8,128)(2,1)}, bf16[1,512,8,64]{1,3,2,0:T(8,128)(2,1)S(1)}, u32[]{:S(2)}, u32[]{:S(2)}) collective-permute-start(bf16[1,512,8,64]{1,3,2,0:T(8,128)(2,1)} %get-tuple-element.706), channel_id=1, source_target_pairs={{0,1},{1,2},{2,3},{3,4},{4,5},{5,6},{6,7},{7,8},{8,9},{9,10},{10,1... | collective-permute-start | bytes 1572872 | tf_op jit(solution)/shard_map/while/body/eval_jaxpr/ppermute | solution.py:141
  1067.5 52.3 %collective-permute-start.5 = (f32[1,512,8,64]{1,3,2,0:T(8,128)}, f32[1,512,8,64]{1,3,2,0:T(8,128)}, u32[]{:S(2)}, u32[]{:S(2)}) collective-permute-start(f32[1,512,8,64]{1,3,2,0:T(8,128)} %get-tuple-element.709), channel_id=1, source_target_pairs={{0,1},{1,2},{2,3},{3,4},{4,5},{5,6},{6,7},{7,8},{8,9},{9,10},{10,1... | collective-permute-start | bytes 3145736 | tf_op jit(solution)/shard_map/while/body/eval_jaxpr/ppermute | solution.py:141
  1067.5 52.3 %collective-permute-start.4 = (f32[1,512,8,64]{1,3,2,0:T(8,128)}, f32[1,512,8,64]{1,3,2,0:T(8,128)}, u32[]{:S(2)}, u32[]{:S(2)}) collective-permute-start(f32[1,512,8,64]{1,3,2,0:T(8,128)} %get-tuple-element.708), channel_id=1, source_target_pairs={{0,1},{1,2},{2,3},{3,4},{4,5},{5,6},{6,7},{7,8},{8,9},{9,10},{10,1... | collective-permute-start | bytes 3145736 | tf_op jit(solution)/shard_map/while/body/eval_jaxpr/ppermute | solution.py:141
  1067.5 49.6 %collective-permute-start.3 = (bf16[1,512,8,64]{1,3,2,0:T(8,128)(2,1)}, bf16[1,512,8,64]{1,3,2,0:T(8,128)(2,1)}, u32[]{:S(2)}, u32[]{:S(2)}) collective-permute-start(bf16[1,512,8,64]{1,3,2,0:T(8,128)(2,1)} %get-tuple-element.707), channel_id=1, source_target_pairs={{0,1},{1,2},{2,3},{3,4},{4,5},{5,6},{6,7},{7,8},{8,9},{9,10},{10,1... | collective-permute-start | bytes 1572872 | tf_op jit(solution)/shard_map/while/body/eval_jaxpr/ppermute | solution.py:141
  1067.5 51.4 %collective-permute-start.2 = (bf16[1,512,8,64]{1,3,2,0:T(8,128)(2,1)}, bf16[1,512,8,64]{1,3,2,0:T(8,128)(2,1)S(1)}, u32[]{:S(2)}, u32[]{:S(2)}) collective-permute-start(bf16[1,512,8,64]{1,3,2,0:T(8,128)(2,1)} %get-tuple-element.706), channel_id=1, source_target_pairs={{0,1},{1,2},{2,3},{3,4},{4,5},{5,6},{6,7},{7,8},{8,9},{9,10},{10,1... | collective-permute-start | bytes 1572872 | tf_op jit(solution)/shard_map/while/body/eval_jaxpr/ppermute | solution.py:141
  1124.3 52.3 %collective-permute-start.5 = (f32[1,512,8,64]{1,3,2,0:T(8,128)}, f32[1,512,8,64]{1,3,2,0:T(8,128)}, u32[]{:S(2)}, u32[]{:S(2)}) collective-permute-start(f32[1,512,8,64]{1,3,2,0:T(8,128)} %get-tuple-element.709), channel_id=1, source_target_pairs={{0,1},{1,2},{2,3},{3,4},{4,5},{5,6},{6,7},{7,8},{8,9},{9,10},{10,1... | collective-permute-start | bytes 3145736 | tf_op jit(solution)/shard_map/while/body/eval_jaxpr/ppermute | solution.py:141
  1124.3 52.3 %collective-permute-start.4 = (f32[1,512,8,64]{1,3,2,0:T(8,128)}, f32[1,512,8,64]{1,3,2,0:T(8,128)}, u32[]{:S(2)}, u32[]{:S(2)}) collective-permute-start(f32[1,512,8,64]{1,3,2,0:T(8,128)} %get-tuple-element.708), channel_id=1, source_target_pairs={{0,1},{1,2},{2,3},{3,4},{4,5},{5,6},{6,7},{7,8},{8,9},{9,10},{10,1... | collective-permute-start | bytes 3145736 | tf_op jit(solution)/shard_map/while/body/eval_jaxpr/ppermute | solution.py:141
  1124.3 49.6 %collective-permute-start.3 = (bf16[1,512,8,64]{1,3,2,0:T(8,128)(2,1)}, bf16[1,512,8,64]{1,3,2,0:T(8,128)(2,1)}, u32[]{:S(2)}, u32[]{:S(2)}) collective-permute-start(bf16[1,512,8,64]{1,3,2,0:T(8,128)(2,1)} %get-tuple-element.707), channel_id=1, source_target_pairs={{0,1},{1,2},{2,3},{3,4},{4,5},{5,6},{6,7},{7,8},{8,9},{9,10},{10,1... | collective-permute-start | bytes 1572872 | tf_op jit(solution)/shard_map/while/body/eval_jaxpr/ppermute | solution.py:141
  1124.3 51.4 %collective-permute-start.2 = (bf16[1,512,8,64]{1,3,2,0:T(8,128)(2,1)}, bf16[1,512,8,64]{1,3,2,0:T(8,128)(2,1)S(1)}, u32[]{:S(2)}, u32[]{:S(2)}) collective-permute-start(bf16[1,512,8,64]{1,3,2,0:T(8,128)(2,1)} %get-tuple-element.706), channel_id=1, source_target_pairs={{0,1},{1,2},{2,3},{3,4},{4,5},{5,6},{6,7},{7,8},{8,9},{9,10},{10,1... | collective-permute-start | bytes 1572872 | tf_op jit(solution)/shard_map/while/body/eval_jaxpr/ppermute | solution.py:141
  1181.1 47.4 %collective-permute-start.6 = (f32[1,512,8,64]{1,3,2,0:T(8,128)}, f32[1,512,8,64]{1,3,2,0:T(8,128)S(1)}, u32[]{:S(2)}, u32[]{:S(2)}) collective-permute-start(f32[1,512,8,64]{1,3,2,0:T(8,128)} %get-tuple-element.420), channel_id=1, source_target_pairs={{0,1},{1,2},{2,3},{3,4},{4,5},{5,6},{6,7},{7,8},{8,9},{9,10},{10,1... | collective-permute-start | bytes 3145736 | tf_op jit(solution)/shard_map/ppermute | solution.py:153
  1181.1 49.0 %collective-permute-start.7 = (f32[1,512,8,64]{1,3,2,0:T(8,128)}, f32[1,512,8,64]{1,3,2,0:T(8,128)S(1)}, u32[]{:S(2)}, u32[]{:S(2)}) collective-permute-start(f32[1,512,8,64]{1,3,2,0:T(8,128)} %get-tuple-element.421), channel_id=1, source_target_pairs={{0,1},{1,2},{2,3},{3,4},{4,5},{5,6},{6,7},{7,8},{8,9},{9,10},{10,1... | collective-permute-start | bytes 3145736 | tf_op jit(solution)/shard_map/ppermute | solution.py:153
  (125 other events, 6499.9 us)
Sparse Core Ops, SparseCore 0:
  1234.1 202.6 all-reduce.3
where the time goes:
time: 1470 us; the launch traced here: 1460 us
  waiting for transfers between devices  644 us (44%)
  starting transfers between devices  422 us (29%)
  local copies, waits for them, and re-layouts  176 us (12%)
  blocking collectives  95.3 us (6%)
  matrix products  79.5 us (5%)
  other arithmetic  22.4 us (2%)
  between operations  15.4 us (1%)
    ppermute x60, waiting for transfers between devices, bwd_step(): lax.ppermute((k_cur, v_cur, dk_cur, dv_cur), 'cp', shift_perm)  373 us
    ppermute x60, starting transfers between devices, bwd_step(): lax.ppermute((k_cur, v_cur, dk_cur, dv_cur), 'cp', shift_perm)  297 us
    ppermute x30, waiting for transfers between devices, fwd_step(): k_cur, v_cur = lax.ppermute((k_cur, v_cur), 'cp', shift_perm)  158 us
    while x90, local copies, waits for them, and re-layouts  148 us
    ppermute x30, starting transfers between devices, fwd_step(): k_cur, v_cur = lax.ppermute((k_cur, v_cur), 'cp', shift_perm)  125 us
    psum x1, blocking collectives, local_layer(): lax.psum((d_ln1_gain, d_ln1_bias, d_ln2_gain, d_ln2_bias, d_w_qkv, d_b_qk...  95.3 us
    psum x1, waiting for transfers between devices, local_layer(): lax.psum((d_ln1_gain, d_ln1_bias, d_ln2_gain, d_ln2_bias, d_w_qkv, d_b_qk...  90.1 us
  transfers between devices with their start and end apart: 93, of which 48 were waited for; matrix products, arithmetic and copies ran while one was open for 5% of the time, Pallas kernels for 0%

commit v1 on v0

v1 whole, which is shorter than its diff:
```python
import functools
import math

import jax
import jax.numpy as jnp
from jax import lax
from jax.experimental import pallas as pl
from jax.experimental.pallas import tpu as pltpu
from jax.sharding import PartitionSpec as P

EPS = 1e-5
ROPE_BASE = 10000.0
NEG_BIG = -1e30
LOG2E = math.log2(math.e)
F32 = jnp.float32
BF16 = jnp.bfloat16


def dot(a, b):
    return jnp.dot(a, b, preferred_element_type=F32)


def dot_nt(a, b):
    return lax.dot_general(a, b, (((1,), (1,)), ((), ())), preferred_element_type=F32)


def layer_norm(row_vals, norm_gain, norm_shift):
    row_mean = jnp.mean(row_vals, axis=-1, keepdims=True)
    centered = row_vals - row_mean
    inv_std = lax.rsqrt(jnp.mean(centered * centered, axis=-1, keepdims=True) + EPS)
    x_norm = centered * inv_std
    return x_norm * norm_gain + norm_shift, x_norm, inv_std


def norm_backward(d_out, x_norm, inv_std, norm_gain):
    d_norm = d_out * norm_gain
    d_rows = inv_std * (d_norm - jnp.mean(d_norm, axis=-1, keepdims=True) - x_norm * jnp.mean(d_norm * x_norm, axis=-1, keepdims=True))
    return d_rows, jnp.sum(d_out * x_norm, axis=0), jnp.sum(d_out, axis=0)


def rope_tables(positions, head_dim):
    rot_dim = head_dim // 4
    inv_freq = ROPE_BASE ** (-2.0 * jnp.arange(rot_dim // 2, dtype=F32) / rot_dim)
    angles = inv_freq[:, None] * positions.astype(F32)[None, :]
    return jnp.cos(angles), jnp.sin(angles)


def rotate_t(head_vals, cos_t, sin_t):
    half = cos_t.shape[0]
    first = head_vals[:half]
    second = head_vals[half:2 * half]
    return jnp.concatenate([first * cos_t - second * sin_t, second * cos_t + first * sin_t, head_vals[2 * half:]], axis=0)


def pre_kernel(x_ref, gain_ref, bias_ref, w_ref, b_ref, cos_ref, sin_ref, h_ref, q_ref, k_ref, v_ref, kn_ref):
    head_dim = q_ref.shape[0]
    h_rows = layer_norm(x_ref[...].astype(F32), gain_ref[...], bias_ref[...])[0].astype(BF16)
    h_ref[...] = h_rows
    qkv = dot_nt(w_ref[...], h_rows) + b_ref[...]
    cos_t, sin_t = cos_ref[...], sin_ref[...]
    q_ref[...] = rotate_t(qkv[:head_dim], cos_t, sin_t).astype(BF16)
    k_t = rotate_t(qkv[head_dim:2 * head_dim], cos_t, sin_t)
    k_ref[...] = k_t.astype(BF16)
    kn_ref[...] = k_t.T.astype(BF16)
    v_ref[...] = qkv[2 * head_dim:].astype(BF16)


def pre_call(x_all, gain, bias, w_head, b_head, cos_t, sin_t, rows):
    seq, width = x_all.shape
    head_dim = w_head.shape[0] // 3
    half = cos_t.shape[0]
    whole = lambda shape: pl.BlockSpec(shape, lambda i: (0,) * len(shape))
    cols = lambda n: pl.BlockSpec((n, rows), lambda i: (0, i))
    return pl.pallas_call(
        pre_kernel,
        grid=(seq // rows,),
        in_specs=[pl.BlockSpec((rows, width), lambda i: (i, 0)), whole((1, width)), whole((1, width)),
                  whole(w_head.shape), whole(b_head.shape), cols(half), cols(half)],
        out_specs=[pl.BlockSpec((rows, width), lambda i: (i, 0)), cols(head_dim), cols(head_dim), cols(head_dim),
                   pl.BlockSpec((rows, head_dim), lambda i: (i, 0))],
        out_shape=[jax.ShapeDtypeStruct((seq, width), BF16)] + [jax.ShapeDtypeStruct((head_dim, seq), BF16)] * 3
        + [jax.ShapeDtypeStruct((seq, head_dim), BF16)],
        cost_estimate=pl.CostEstimate(flops=2 * seq * width * w_head.shape[0] * 3, bytes_accessed=seq * width * 4, transcendentals=0),
        name="pre",
    )(x_all, gain, bias, w_head, b_head, cos_t, sin_t)


def fwd_kernel(core_ref, kn_ref, q_ref, v_ref, ctx_ref, norm_ref, lse_ref, max_s, sum_s, acc_s, *, par, sub, scale2):
    step = pl.program_id(0)
    core = core_ref[0]
    rows = q_ref.shape[1]
    span = par * rows
    q_t = q_ref[...]

    def chunk(start, masked, first):
        score_list = []
        for j in range(span // sub):
            keys = kn_ref[pl.ds(pl.multiple_of(start + j * sub, sub), sub), :]
            scores = dot(keys, q_t)
            if masked:
                key_pos = j * sub + lax.broadcasted_iota(jnp.int32, scores.shape, 0)
                q_pos = core * rows + lax.broadcasted_iota(jnp.int32, scores.shape, 1)
                scores = jnp.where(key_pos <= q_pos, scores, NEG_BIG)
            score_list.append(scores)
        for j, scores in enumerate(score_list):
            blk_max = jnp.max(scores, axis=0, keepdims=True) * scale2
            fresh = first and j == 0
            old_max = None if fresh else max_s[...]
            new_max = blk_max if fresh else jnp.maximum(old_max, blk_max)
            probs = jnp.exp2(scores * scale2 - new_max)
            vals = v_ref[:, pl.ds(pl.multiple_of(start + j * sub, sub), sub)]
            part = dot(vals, probs.astype(BF16))
            part_sum = jnp.sum(probs, axis=0, keepdims=True)
            if fresh:
                sum_s[...] = part_sum
                acc_s[...] = part
            else:
                alpha = jnp.exp2(old_max - new_max)
                sum_s[...] = sum_s[...] * alpha + part_sum
                acc_s[...] = acc_s[...] * alpha + part
            max_s[...] = new_max

    chunk(step * span, True, True)

    @pl.loop(0, step)
    def _(i):
        chunk(i * span, False, False)

    total = sum_s[...]
    normed = acc_s[...] / total
    norm_ref[0] = normed
    ctx_ref[0] = normed.astype(BF16)
    lse_ref[0] = max_s[...] + jnp.log2(total)


def fwd_call(core, k_nat, q_t, v_t, rows, par, scale2):
    seq, head_dim = k_nat.shape
    steps = seq // (rows * par)
    sub = min(256, rows)
    pick = lambda i, core_ref: (0, i * par + core_ref[0])
    tile = lambda n: pl.BlockSpec((1, n, rows), lambda i, core_ref: (i, 0, 0))
    return pl.pallas_call(
        functools.partial(fwd_kernel, par=par, sub=sub, scale2=scale2),
        grid_spec=pltpu.PrefetchScalarGridSpec(
            num_scalar_prefetch=1, grid=(steps,),
            in_specs=[pl.BlockSpec((seq, head_dim), lambda i, core_ref: (0, 0)), pl.BlockSpec((head_dim, rows), pick),
                      pl.BlockSpec((head_dim, seq), lambda i, core_ref: (0, 0))],
            out_specs=[tile(head_dim), tile(head_dim), tile(1)],
            scratch_shapes=[pltpu.VMEM((1, rows), F32), pltpu.VMEM((1, rows), F32), pltpu.VMEM((head_dim, rows), F32)]),
        out_shape=[jax.ShapeDtypeStruct((steps, head_dim, rows), BF16), jax.ShapeDtypeStruct((steps, head_dim, rows), F32),
                   jax.ShapeDtypeStruct((steps, 1, rows), F32)],
        cost_estimate=pl.CostEstimate(flops=32 * seq * seq * head_dim // par, bytes_accessed=seq * head_dim * 8, transcendentals=seq * seq // 4),
        name="attn_fwd",
    )(core, k_nat, q_t, v_t)


def bwd_kernel(core_ref, k_ref, kn_ref, v_ref, q_ref, dy_ref, w_ref, ctx_ref, norm_ref, lse_ref,
               dq_ref, dk_ref, dv_ref, dw_ref, dq_s, *, par, sub, scale, scale2):
    step = pl.program_id(0)
    core = core_ref[0]
    rows = q_ref.shape[1]
    subs = rows // sub

    @pl.when(step == 0)
    def _():
        dk_ref[...] = jnp.zeros_like(dk_ref)
        dv_ref[...] = jnp.zeros_like(dv_ref)
        dw_ref[...] = jnp.zeros_like(dw_ref)

    q_t = q_ref[...]
    q_n = q_t.T
    dy_rows = dy_ref[0]
    d_ctx = dot_nt(w_ref[...], dy_rows)
    delta = jnp.sum(d_ctx * norm_ref[0], axis=0, keepdims=True)
    do_t = d_ctx.astype(BF16)
    do_n = do_t.T
    dw_ref[...] += dot(ctx_ref[0], dy_rows)
    lanes = 128
    spread = lambda row: jnp.concatenate([jnp.broadcast_to(row, (lanes, rows)).T] * (sub // lanes), axis=1)
    lse_c = spread(lse_ref[0])
    delta_c = spread(delta)
    dq_s[...] = jnp.zeros_like(dq_s)

    def chunk(i, masked):
        for b in range(par):
            for j in range(subs):
                cols = slice(j * sub, (j + 1) * sub)
                start = pl.multiple_of((i * par + b) * rows + j * sub, sub)
                k_t = k_ref[:, pl.ds(start, sub)]
                v_t = v_ref[:, pl.ds(start, sub)]
                probs = jnp.exp2(dot(q_n, k_t) * scale2 - lse_c)
                if masked:
                    key_pos = b * rows + j * sub + lax.broadcasted_iota(jnp.int32, probs.shape, 1)
                    q_pos = core * rows + lax.broadcasted_iota(jnp.int32, probs.shape, 0)
                    probs = jnp.where(key_pos <= q_pos, probs, 0.0)
                d_scores = (probs * (dot(do_n, v_t) - delta_c)).astype(BF16)
                dv_ref[i * par + b, :, cols] += dot(do_t, probs.astype(BF16))
                dk_ref[i * par + b, :, cols] += dot(q_t, d_scores)
                dq_s[...] += dot(d_scores, kn_ref[pl.ds(start, sub), :])

    chunk(step, True)

    @pl.loop(0, step)
    def _(i):
        chunk(i, False)

    dq_ref[0] = dq_s[...].T * scale


def bwd_call(core, k_t, k_nat, v_t, q_t, dy_all, w_head, ctx_t, norm_t, lse, rows, par, scale, scale2):
    seq, head_dim = k_nat.shape
    width = dy_all.shape[-1]
    steps = seq // (rows * par)
    sub = min(256, rows)
    whole = lambda shape: pl.BlockSpec(shape, lambda i, core_ref: (0,) * len(shape))
    tile = lambda n: pl.BlockSpec((1, n, rows), lambda i, core_ref: (i, 0, 0))
    return pl.pallas_call(
        functools.partial(bwd_kernel, par=par, sub=sub, scale=scale, scale2=scale2),
        grid_spec=pltpu.PrefetchScalarGridSpec(
            num_scalar_prefetch=1, grid=(steps,),
            in_specs=[whole((head_dim, seq)), whole((seq, head_dim)), whole((head_dim, seq)),
                      pl.BlockSpec((head_dim, rows), lambda i, core_ref: (0, i * par + core_ref[0])),
                      pl.BlockSpec((1, rows, width), lambda i, core_ref: (i * par + core_ref[0], 0, 0)),
                      whole((head_dim, width)), tile(head_dim), tile(head_dim), tile(1)],
            out_specs=[tile(head_dim), whole((steps * par, head_dim, rows)), whole((steps * par, head_dim, rows)), whole((head_dim, width))],
            scratch_shapes=[pltpu.VMEM((rows, head_dim), F32)]),
        out_shape=[jax.ShapeDtypeStruct((steps, head_dim, rows), F32), jax.ShapeDtypeStruct((steps * par, head_dim, rows), F32),
                   jax.ShapeDtypeStruct((steps * par, head_dim, rows), F32), jax.ShapeDtypeStruct((head_dim, width), F32)],
        cost_estimate=pl.CostEstimate(flops=64 * seq * seq * head_dim // par, bytes_accessed=seq * head_dim * 32, transcendentals=seq * seq // 4),
        name="attn_bwd",
    )(core, k_t, k_nat, v_t, q_t, dy_all.reshape(-1, rows, width), w_head, ctx_t, norm_t, lse)


def exact_gelu(pre_act):
    return jax.nn.gelu(pre_act, approximate=False)


def solution(mesh):
    cp_size = mesh.shape['cp']
    row_spec = P('dp', 'cp', None)
    in_specs = (row_spec, row_spec) + (P(),) * 12
    out_specs = (row_spec, row_spec, P('dp'), P('dp'), P('dp'), P('dp'), P('dp', None, None, None), P('dp', None, None), P('dp', None), P('dp'), P('dp', None), P('dp'), P('dp', None), P('dp'))

    def local_layer(x_blk, dy_blk, ln1_gain, ln1_bias, ln2_gain, ln2_bias, w_qkv, b_qkv, w_out, b_out, w_up, b_up, w_down, b_down):
        rows, width = x_blk.shape[1], x_blk.shape[2]
        heads, head_dim = w_qkv.shape[1], w_qkv.shape[3]
        par = cp_size // heads
        seq = rows * cp_size
        scale = head_dim ** -0.5
        scale2 = scale * LOG2E
        me = lax.axis_index('cp')
        head, core = me // par, me % par
        core_arr = jnp.reshape(core, (1,)).astype(jnp.int32)
        same_core = [[z * par + c for z in range(heads)] for c in range(par)]
        x_own, dy_own = x_blk[0], dy_blk[0]
        dy_bf = dy_own.astype(BF16)

        x_all = lax.all_gather(x_own, 'cp', tiled=True)
        dy_all = lax.all_gather(dy_bf, 'cp', tiled=True)

        x_rows = x_own.astype(F32)
        h_mlp, x_norm, inv_std = layer_norm(x_rows, ln2_gain, ln2_bias)
        h_mlp = h_mlp.astype(BF16)
        up_proj = dot(h_mlp, w_up) + b_up.astype(F32)
        gelu_out, gelu_back = jax.vjp(exact_gelu, up_proj)
        gelu_bf = gelu_out.astype(BF16)
        mlp_proj = dot(gelu_bf, w_down) + b_down.astype(F32)
        dy_sum = jnp.sum(dy_own, axis=0)
        d_w_down = dot(gelu_bf.T, dy_bf)
        d_up = gelu_back(dot_nt(dy_bf, w_down))[0]
        d_b_up = jnp.sum(d_up, axis=0)
        d_up_bf = d_up.astype(BF16)
        d_w_up = dot(h_mlp.T, d_up_bf)
        d_h_mlp = dot_nt(d_up_bf, w_up)
        dx_mlp, d_ln2_gain, d_ln2_bias = norm_backward(d_h_mlp, x_norm, inv_std, ln2_gain)
        early = lax.psum((d_w_up, d_w_down, d_b_up, dy_sum, d_ln2_gain, d_ln2_bias), 'cp')

        cos_t, sin_t = rope_tables(jnp.arange(seq), head_dim)
        w_head = lax.dynamic_index_in_dim(w_qkv, head, axis=1, keepdims=False).reshape(width, 3 * head_dim).T
        b_head = lax.dynamic_index_in_dim(b_qkv, head, axis=0, keepdims=False).reshape(3 * head_dim, 1).astype(F32)
        wo_head = lax.dynamic_slice_in_dim(w_out, head * head_dim, head_dim, axis=0)
        h_all, q_t, k_t, v_t, k_nat = pre_call(x_all, ln1_gain[None], ln1_bias[None], w_head, b_head, cos_t, sin_t, rows)
        ctx_t, norm_t, lse = fwd_call(core_arr, k_nat, q_t, v_t, rows, par, scale2)

        ctx_mine = lax.all_to_all(ctx_t, 'cp', 0, 0, axis_index_groups=same_core, tiled=True).reshape(width, rows)
        attn_proj = dot(ctx_mine.T, w_out) + b_out.astype(F32)
        y_rows = (x_rows + attn_proj + mlp_proj).astype(BF16)

        d_q, dk_part, dv_part, dwo_part = bwd_call(core_arr, k_t, k_nat, v_t, q_t, dy_all, wo_head, ctx_t, norm_t, lse, rows, par, scale, scale2)
        dkv_part = jnp.stack([dk_part, dv_part]).reshape(2, heads, par, head_dim, rows)
        other = lax.dynamic_index_in_dim(dkv_part, par - 1 - core, axis=2, keepdims=False)
        mine = lax.dynamic_index_in_dim(dkv_part, core, axis=2, keepdims=False)
        swap = [(z * par + c, z * par + par - 1 - c) for z in range(heads) for c in range(par)]
        d_k, d_v = mine + lax.ppermute(other, 'cp', swap)
        d_k = d_k * scale
        own_cos = lax.dynamic_index_in_dim(cos_t.reshape(-1, heads, par, rows), core, axis=2, keepdims=False)
        own_sin = lax.dynamic_index_in_dim(sin_t.reshape(-1, heads, par, rows), core, axis=2, keepdims=False)
        unrotate = jax.vmap(rotate_t, in_axes=(0, 1, 1))
        d_qkv = jnp.concatenate([unrotate(d_q, own_cos, -own_sin), unrotate(d_k, own_cos, -own_sin), d_v], axis=1)
        d_b_head = jnp.sum(d_qkv, axis=(0, 2))
        d_qkv = d_qkv.astype(BF16)
        d_qkv_mine = lax.all_to_all(d_qkv, 'cp', 0, 0, axis_index_groups=same_core, tiled=True).reshape(heads * 3 * head_dim, rows)
        d_h = lax.dot_general(d_qkv_mine, w_qkv.reshape(width, -1), (((0,), (1,)), ((), ())), preferred_element_type=F32)
        x_norm1 = x_norm
        dx_attn, d_ln1_gain, d_ln1_bias = norm_backward(d_h, x_norm1, inv_std, ln1_gain)
        dx_rows = dy_own + dx_attn + dx_mlp

        h_own = lax.dynamic_index_in_dim(h_all.reshape(heads, par, rows, width), core, axis=1, keepdims=False)
        d_w_head = jnp.einsum('ztd,zet->de', h_own, d_qkv, preferred_element_type=F32)
        d_w_full = jnp.zeros((width, heads, 3 * head_dim), F32)
        d_w_full = lax.dynamic_update_slice(d_w_full, d_w_head[:, None], (0, head, 0)).reshape(w_qkv.shape)
        d_b_full = lax.dynamic_update_slice(jnp.zeros((heads, 3 * head_dim), F32), d_b_head[None], (head, 0)).reshape(b_qkv.shape)
        d_wo_full = lax.dynamic_update_slice(jnp.zeros((width, width), F32), dwo_part, (head * head_dim, 0))
        late, early = lax.optimization_barrier(((d_w_full, d_b_full, d_wo_full, d_ln1_gain, d_ln1_bias), early))
        d_w_up, d_w_down, d_b_up, dy_sum, d_ln2_gain, d_ln2_bias = early
        d_w_qkv, d_b_qkv, d_w_out, d_ln1_gain, d_ln1_bias = lax.psum(late, 'cp')
        return (y_rows[None], dx_rows[None], d_ln1_gain, d_ln1_bias, d_ln2_gain, d_ln2_bias, d_w_qkv, d_b_qkv, d_w_out, dy_sum, d_w_up, d_b_up, d_w_down, dy_sum)

    return jax.shard_map(local_layer, mesh=mesh, in_specs=in_specs, out_specs=out_specs, check_vma=False)
```

time: 1470 us -> 513 us (0.35)
  waiting for transfers between devices: 644 us -> 177 us
  starting transfers between devices: 422 us -> 11.1 us
  local copies, waits for them, and re-layouts: 176 us -> 21.9 us
  Pallas kernels: 0 us -> 131 us
  matrix products: 79.5 us -> 42.3 us
    ppermute x92 -> x1, waiting for transfers between devices: 554 us -> 0.01 us  [local_layer(): d_k, d_v = mine + lax.ppermute(other, 'cp', swap)]
    ppermute x92 -> x1, starting transfers between devices: 422 us -> 0.27 us  [local_layer(): d_k, d_v = mine + lax.ppermute(other, 'cp', swap)]
    while x90 -> x0, local copies, waits for them, and re-layouts: 148 us -> none
    pallas_call x0 -> x3, Pallas kernels: none -> 131 us  [the longest x1 73.1 us: bwd_call(): pl.pallas_call(functools.partial(bwd_kernel, par=par, sub=sub, scale=scal...]
    all_to_all x0 -> x2, waiting for transfers between devices: none -> 48.4 us  [the longest x1 35.3 us: local_layer(): lax.all_to_all(d_qkv, 'cp', 0, 0, axis_index_groups=same_core, tiled=True)]
    dot_general x23 -> x9, matrix products: 73.9 us -> 42.3 us  [the longest x2 17.3 us: dot_nt(): lax.dot_general(a, b, (((1,), (1,)), ((), ())), preferred_element_type=F32)]
    all_gather x0 -> x2, waiting for transfers between devices: none -> 31.4 us  [the longest x1 31.4 us: local_layer(): x_all = lax.all_gather(x_own, 'cp', tiled=True)]
    psum x1 -> x2, blocking collectives: 95.3 us -> 88.8 us  [the longest x1 45.5 us: local_layer(): d_w_qkv, d_b_qkv, d_w_out, d_ln1_gain, d_ln1_bias = lax.psum(late, 'cp')]
  transfers between devices with their start and end apart: 93 -> 7, of which waited for: 48 -> 5; matrix products, arithmetic and copies ran while one was open for 5% -> 15% of each run, Pallas kernels for 0% -> 11%
where the time goes in v1:
time: 513 us; the launch traced here: 512 us
  waiting for transfers between devices  177 us (35%)
  Pallas kernels  131 us (26%)
  blocking collectives  88.8 us (17%)
  matrix products  42.3 us (8%)
  other arithmetic  25.6 us (5%)
  local copies, waits for them, and re-layouts  21.9 us (4%)
  between operations  14.2 us (3%)
  starting transfers between devices  11.1 us (2%)
    pallas_call x1, Pallas kernels, bwd_call(): pl.pallas_call(functools.partial(bwd_kernel, par=par, sub=sub, scale=scal...  73.1 us
    psum x1, waiting for transfers between devices, local_layer(): d_w_qkv, d_b_qkv, d_w_out, d_ln1_gain, d_ln1_bias = lax.psum(late, 'cp')  48.8 us
    psum x1, waiting for transfers between devices, local_layer(): lax.psum((d_w_up, d_w_down, d_b_up, dy_sum, d_ln2_gain, d_ln2_bias), 'cp')  47 us
    psum x1, blocking collectives, local_layer(): d_w_qkv, d_b_qkv, d_w_out, d_ln1_gain, d_ln1_bias = lax.psum(late, 'cp')  45.5 us
    psum x1, blocking collectives, local_layer(): lax.psum((d_w_up, d_w_down, d_b_up, dy_sum, d_ln2_gain, d_ln2_bias), 'cp')  43.3 us
    pallas_call x1, Pallas kernels, fwd_call(): pl.pallas_call(functools.partial(fwd_kernel, par=par, sub=sub, scale2=sca...  40.8 us
    all_to_all x1, waiting for transfers between devices, local_layer(): lax.all_to_all(d_qkv, 'cp', 0, 0, axis_index_groups=same_core, tiled=True)  35.3 us
    all_gather x1, waiting for transfers between devices, local_layer(): x_all = lax.all_gather(x_own, 'cp', tiled=True)  31.4 us
  transfers between devices with their start and end apart: 7, of which 5 were waited for; matrix products, arithmetic and copies ran while one was open for 15% of the time, Pallas kernels for 11%

profile of v1, /device:TPU:21, one launch (start us, length us, event | category | flops | bytes accessed | tf_op | source)
XLA Modules:
  0.0 511.7 jit_solution(11611884538340448388)
XLA Ops:
  7.3 0.7 all-gather.6.cloned.1.call-update
  8.1 2.7 fusion.71
  10.9 0.7 fusion.64
  11.7 0.8 reshape.159.b_ref
  12.4 0.7 convert_element_type.55
  13.2 1.5 constant_dynamic-slice_fusion.w_ref
  14.6 1.6 constant_dynamic-slice_fusion.2
  16.2 1.2 convert_reduce_fusion
  17.9 2.9 fusion.66
  20.9 2.1 multiply_sine_fusion
  23.0 12.8 %fusion.68 = (f32[2048]{0:T(1024)}, bf16[512,2048]{1,0:T(8,128)(2,1)}, f32[512,2048]{1,0:T(8,128)}) fusion(f32[512,2048]{1,0:T(8,128)S(1)} %fusion.66, f32[2048]{0:T(1024)S(1)} %convert_element_type.55, bf16[512,512]{1,0:T(8,128)(2,1)S(1)} %copy-done.5, bf16[2048,512]{1,0:T(8,128)(2,1)S(1)} %copy-done), kind=kOutput, calls=%fused_computation.114 | convolution fusion | flops 1151334400 | bytes 13123584 | tf_op jit(solution)/shard_map/dot_general | solution.py:24
  35.8 31.4 %all-gather.6.cloned.1.call-done = bf16[1,8192,512]{2,1,0:T(8,128)(2,1)} async-done(((bf16[1,512,512]{2,1,0:T(8,128)(2,1)}), bf16[1,8192,512]{2,1,0:T(8,128)(2,1)}) %all-gather.6.cloned.1.call-update) | async-done | bytes 8388624 | tf_op jit(solution)/shard_map/all_gather | solution.py:258
  67.2 17.3 %pre.1 = (bf16[8192,512]{1,0:T(8,128)(2,1)}, bf16[64,8192]{1,0:T(8,128)(2,1)}, bf16[64,8192]{1,0:T(8,128)(2,1)}, bf16[64,8192]{1,0:T(8,128)(2,1)}, bf16[8192,64]{1,0:T(8,128)(2,1)}) custom-call(bf16[8192,512]{1,0:T(8,128)(2,1)} %bitcast.170, f32[1,512]{1,0:T(1,128)} %bitcast.168, f32[1,512]{1,0:T(1,128)} %bitcast.171, bf16[192,512]{1,0:T(8,128)(2,1)} %bitcast.165, ...), custom_call_target="tpu_custom_call" | custom-call | flops 4831838208 | bytes 16777216 | tf_op jit(solution)/shard_map/pre/pallas_call | solution.py:74
  84.6 40.8 %attn_fwd.1 = (bf16[8,64,512]{2,1,0:T(8,128)(2,1)}, f32[8,64,512]{2,1,0:T(8,128)}, f32[8,1,512]{2,1,0:T(1,128)}) custom-call(s32[1]{0:T(128)} %bitcast.1.core_ref, bf16[8192,64]{1,0:T(8,128)(2,1)} %get-tuple-element.37.kn_ref, bf16[64,8192]{1,0:T(8,128)(2,1)} %get-tuple-element.38.q_ref, bf16[64,8192]{1,0:T(8,128)(2,1)} %get-tuple-element.39.v_ref), custom_call_target="tpu_custom_call" | custom-call | flops 68719476736 | bytes 4194304 | tf_op jit(solution)/shard_map/attn_fwd/pallas_call | solution.py:142
  125.4 73.1 %attn_bwd.1 = (f32[8,64,512]{2,1,0:T(8,128)}, f32[16,64,512]{2,1,0:T(8,128)}, f32[16,64,512]{2,1,0:T(8,128)}, f32[64,512]{1,0:T(8,128)}) custom-call(s32[1]{0:T(128)} %bitcast.1.core_ref, bf16[64,8192]{1,0:T(8,128)(2,1)} %get-tuple-element.41.k_ref, bf16[8192,64]{1,0:T(8,128)(2,1)} %get-tuple-element.37.kn_ref, bf16[64,8192]{1,0:T(8,128)(2,1)} %get-tuple-element.39.v_ref, ...), custom_call_target="tpu_custom_call" | custom-call | flops 137438953472 | bytes 16777216 | tf_op jit(solution)/shard_map/attn_bwd/pallas_call | solution.py:217
  198.4 3.2 fusion.10
  202.0 3.2 multiply_convert_fusion
  205.3 3.3 fusion.72
  208.7 3.5 fusion.50
  212.9 1.5 fusion.55
  214.3 1.5 fusion.57
  215.8 1.2 slice_dynamic-update-slice_fusion.1
  217.0 2.3 fusion.13
  220.6 1.5 fusion.70
  222.1 4.5 all-to-all-start.1
  226.7 4.5 fusion.52
  231.2 1.1 broadcast_in_dim.50
  232.3 0.7 constant_dynamic-update-slice_fusion
  233.0 2.1 broadcast_in_dim.22
  235.1 4.4 fusion.31
  239.5 35.3 %all-to-all-done.1 = bf16[8,192,512]{2,1,0:T(8,128)(2,1)} async-done(((bf16[8,192,512]{2,1,0:T(8,128)(2,1)}), bf16[8,192,512]{2,1,0:T(8,128)(2,1)}, u32[]{:S(2)}, u32[]{:S(2)}) %all-to-all-start.1) | async-done | bytes 1572896 | tf_op jit(solution)/shard_map/all_to_all | solution.py:302
  274.9 4.4 fusion.45
  279.3 43.3 %all-reduce.1 = (f32[2048]{0:T(1024)}, f32[512]{0:T(512)S(1)}, f32[512]{0:T(512)}, f32[512]{0:T(512)}) all-reduce(f32[2048]{0:T(1024)S(1)} %copy-done.20, f32[512]{0:T(512)S(1)} %copy-done.17, f32[512]{0:T(512)S(1)} %get-tuple-element.85, f32[512]{0:T(512)S(1)} %get-tuple-element.82), channel_id=1, replica_groups=mesh['dp'=4,'cp'=16] {'cp'}, use_global_device_ids=true, to_apply=%region_12.13 | all-reduce | flops 3584 | bytes 28672 | tf_op jit(solution)/shard_map/psum | solution.py:276
  322.6 47.0 %all-reduce.9.cloned.1.call-done = (f32[512,2048]{1,0:T(8,128)}, f32[2048,512]{1,0:T(8,128)}) async-done(((f32[512,2048]{1,0:T(8,128)}, f32[2048,512]{1,0:T(8,128)}), (f32[512,2048]{1,0:T(8,128)}, f32[2048,512]{1,0:T(8,128)})) %all-reduce.9.cloned.1.call-update) | async-done | bytes 8388624 | tf_op jit(solution)/shard_map/psum | solution.py:276
  369.6 6.1 %all-to-all-start = ((bf16[8,64,512]{2,1,0:T(8,128)(2,1)}), bf16[8,64,512]{2,1,0:T(8,128)(2,1)S(1)}, u32[]{:S(2)}, u32[]{:S(2)}) async-start(bf16[8,64,512]{2,1,0:T(8,128)(2,1)} %get-tuple-element.40.ctx_ref), calls=%async_computation | async-start | bytes 1048576 | tf_op jit(solution)/shard_map/all_to_all | solution.py:285
  375.8 3.8 convolution_add_fusion.1
  379.6 13.1 %all-to-all-done = bf16[8,64,512]{2,1,0:T(8,128)(2,1)S(1)} async-done(((bf16[8,64,512]{2,1,0:T(8,128)(2,1)}), bf16[8,64,512]{2,1,0:T(8,128)(2,1)S(1)}, u32[]{:S(2)}, u32[]{:S(2)}) %all-to-all-start) | async-done | bytes 524320 | tf_op jit(solution)/shard_map/all_to_all | solution.py:285
  392.7 2.7 fusion.27
  395.4 45.5 %all-reduce = (f32[512]{0:T(512)}, f32[512]{0:T(512)}, f32[8,3,64]{2,1,0:T(4,128)S(1)}) all-reduce(f32[512]{0:T(512)S(1)} %get-tuple-element.49, f32[512]{0:T(512)S(1)} %get-tuple-element.50, f32[8,3,64]{2,1,0:T(4,128)S(1)} %reshape.154), channel_id=1, replica_groups=mesh['dp'=4,'cp'=16] {'cp'}, use_global_device_ids=true, to_apply=%region_19.20 | all-reduce | flops 2560 | bytes 20480 | tf_op jit(solution)/shard_map/psum | solution.py:316
  440.9 0.6 copy.29
  441.5 3.4 fusion.41
  444.9 48.8 %all-reduce.7.cloned.1.call-done = (f32[512,8,3,64]{0,3,2,1:T(8,128)}, f32[512,512]{1,0:T(8,128)}) async-done(((f32[512,8,3,64]{0,3,2,1:T(8,128)}, f32[512,512]{1,0:T(8,128)}), (f32[512,8,3,64]{0,3,2,1:T(8,128)}, f32[512,512]{1,0:T(8,128)})) %all-reduce.7.cloned.1.call-update) | async-done | bytes 4194320 | tf_op jit(solution)/shard_map/psum | solution.py:316
  493.7 0.6 copy.44
  494.3 4.2 copy.45
  498.5 1.0 copy.46
  499.5 2.1 copy.47
  501.6 1.6 copy-done.7
  503.2 2.0 copy.48
  (92 shorter events, 3.1 us)
Async XLA Ops:
  7.2 15.8 %copy-start = (bf16[2048,512]{1,0:T(8,128)(2,1)S(1)}, bf16[2048,512]{1,0:T(8,128)(2,1)}, u32[]{:S(2)}) copy-start(bf16[2048,512]{1,0:T(8,128)(2,1)} %param.26) | copy-start | bytes 6291460
  7.2 10.3 %copy-start.1 = (bf16[1,512,512]{2,1,0:T(8,128)(2,1)S(1)}, bf16[1,512,512]{2,1,0:T(8,128)(2,1)}, u32[]{:S(2)}) copy-start(bf16[1,512,512]{2,1,0:T(8,128)(2,1)} %param.14) | copy-start | bytes 1572868
  7.2 10.6 %copy-start.21 = (f32[512]{0:T(512)S(1)}, f32[512]{0:T(512)}, u32[]{:S(2)}) copy-start(f32[512]{0:T(512)} %param.18) | copy-start | bytes 6148
  7.2 10.6 %copy-start.29 = (f32[512]{0:T(512)S(1)}, f32[512]{0:T(512)}, u32[]{:S(2)}) copy-start(f32[512]{0:T(512)} %param.19) | copy-start | bytes 6148
  7.2 60.0 %all-gather.6.cloned.1.call-start = ((), (), s32[]{:S(2)}) async-start(), calls=%async_computation.3 | async-start | bytes 8912896 | tf_op jit(solution)/shard_map/all_gather | solution.py:258
  8.0 117.3 %all-gather.4.cloned.1.call-start = ((), (), s32[]{:S(2)}) async-start(), calls=%async_computation.2 | async-start | bytes 8912896 | tf_op jit(solution)/shard_map/all_gather | solution.py:259
  10.8 358.7 %all-reduce.9.cloned.1.call-start = ((), (), s32[]{:S(2)}) async-start(), calls=%async_computation.5 | async-start | bytes 16777216 | tf_op jit(solution)/shard_map/psum | solution.py:276
  13.1 9.9 %copy-start.13 = (f32[2048]{0:T(1024)}, f32[2048]{0:T(1024)S(1)}, u32[]{:S(2)}) copy-start(f32[2048]{0:T(1024)S(1)} %convert_element_type.55) | copy-start | bytes 24580
  13.1 7.7 %copy-start.24 = (f32[8]{0:T(128)}, f32[8]{0:T(128)S(1)}, u32[]{:S(2)}) copy-start(f32[8]{0:T(128)S(1)} %multiply_power_fusion) | copy-start | bytes 100
  16.2 6.8 %copy-start.5 = (bf16[512,512]{1,0:T(8,128)(2,1)S(1)}, bf16[512,512]{1,0:T(8,128)(2,1)}, u32[]{:S(2)}) copy-start(bf16[512,512]{1,0:T(8,128)(2,1)} %get-tuple-element.103) | copy-start | bytes 1572868
  17.5 3.3 copy-start.15
  17.9 3.0 copy-start.18
  20.9 2.2 copy-start.9
  198.4 3.5 copy-start.10
  198.4 3.5 copy-start.14
  201.7 15.3 %collective-permute-start = (f32[2,8,64,512]{3,2,1,0:T(8,128)}, f32[2,8,64,512]{3,2,1,0:T(8,128)}, u32[]{:S(2)}, u32[]{:S(2)}) collective-permute-start(f32[2,8,64,512]{3,2,1,0:T(8,128)} %fusion.10), channel_id=1, source_target_pairs={{0,1},{1,0},{2,3},{3,2},{4,5},{5,4},{6,7},{7,6},{8,9},{9,8},{10,11... | collective-permute-start | bytes 6291464 | tf_op jit(solution)/shard_map/ppermute | solution.py:294
  202.0 3.2 copy-start.6
  205.2 3.4 copy-start.3
  205.2 3.4 copy-start.2
  205.2 3.4 copy-start.16
  205.2 3.4 copy-start.19
  205.3 3.4 copy-start.22
  205.3 3.4 copy-start.30
  205.3 3.4 copy-start.31
  212.1 0.7 copy-start.25
  212.2 4.8 copy-start.4
  222.1 52.7 %all-to-all-start.1 = ((bf16[8,192,512]{2,1,0:T(8,128)(2,1)}), bf16[8,192,512]{2,1,0:T(8,128)(2,1)}, u32[]{:S(2)}, u32[]{:S(2)}) async-start(bf16[8,192,512]{2,1,0:T(8,128)(2,1)} %get-tuple-element.101), calls=%async_computation.1 | async-start | bytes 3145728 | tf_op jit(solution)/shard_map/all_to_all | solution.py:302
  226.6 5.6 %copy-start.12 = (f32[64,512]{1,0:T(8,128)S(1)}, f32[64,512]{1,0:T(8,128)}, u32[]{:S(2)}) copy-start(f32[64,512]{1,0:T(8,128)} %get-tuple-element.48) | copy-start | bytes 393220
  226.6 267.1 %all-reduce.7.cloned.1.call-start = ((), (), s32[]{:S(2)}) async-start(), calls=%async_computation.4 | async-start | bytes 8388608 | tf_op jit(solution)/shard_map/psum | solution.py:316
  235.1 39.7 %copy-start.23 = (f32[512]{0:T(512)S(1)}, f32[512]{0:T(512)}, u32[]{:S(2)}) copy-start(f32[512]{0:T(512)} %param.16) | copy-start | bytes 6148
  274.9 4.4 copy-start.17
  274.9 4.4 copy-start.20
  279.3 96.5 %copy-start.27 = (bf16[512]{0:T(512)(128)(2,1)S(1)}, bf16[512]{0:T(512)(128)(2,1)}, u32[]{:S(2)}) copy-start(bf16[512]{0:T(512)(128)(2,1)} %param.27) | copy-start | bytes 3076
  279.3 96.5 %copy-start.28 = (bf16[512]{0:T(512)(128)(2,1)S(1)}, bf16[512]{0:T(512)(128)(2,1)}, u32[]{:S(2)}) copy-start(bf16[512]{0:T(512)(128)(2,1)} %param.23) | copy-start | bytes 3076
  322.6 171.2 %copy-start.26 = (f32[512]{0:T(512)}, f32[512]{0:T(512)S(1)}, u32[]{:S(2)}) copy-start(f32[512]{0:T(512)S(1)} %get-tuple-element.151) | copy-start | bytes 6148
  369.6 23.1 %all-to-all-start = ((bf16[8,64,512]{2,1,0:T(8,128)(2,1)}), bf16[8,64,512]{2,1,0:T(8,128)(2,1)S(1)}, u32[]{:S(2)}, u32[]{:S(2)}) async-start(bf16[8,64,512]{2,1,0:T(8,128)(2,1)} %get-tuple-element.40.ctx_ref), calls=%async_computation | async-start | bytes 1048576 | tf_op jit(solution)/shard_map/all_to_all | solution.py:285
  493.7 4.8 copy-start.11
  494.3 5.2 %copy-start.8 = (f32[512,2048]{1,0:T(8,128)S(1)}, f32[512,2048]{1,0:T(8,128)}, u32[]{:S(2)}) copy-start(f32[512,2048]{1,0:T(8,128)} %get-tuple-element.152) | copy-start | bytes 12582916
  499.5 3.7 copy-start.7
Sparse Core Ops, SparseCore 0:
  9.7 57.5 all-gather.5
  69.5 51.0 all-gather.3
  212.3 157.2 all-reduce.8
  372.5 121.1 all-reduce.6

commit v2 on v1

--- a/solution.py
+++ b/solution.py
@@ -8,6 +8,7 @@
 from jax.experimental.pallas import tpu as pltpu
 from jax.sharding import PartitionSpec as P
 
+
 EPS = 1e-5
 ROPE_BASE = 10000.0
 NEG_BIG = -1e30
@@ -52,10 +53,12 @@
     return jnp.concatenate([first * cos_t - second * sin_t, second * cos_t + first * sin_t, head_vals[2 * half:]], axis=0)
 
 
-def pre_kernel(x_ref, gain_ref, bias_ref, w_ref, b_ref, cos_ref, sin_ref, h_ref, q_ref, k_ref, v_ref, kn_ref):
+def pre_kernel(x_ref, gain_ref, bias_ref, gain2_ref, bias2_ref, w_ref, b_ref, cos_ref, sin_ref, h_ref, m_ref, q_ref, k_ref, v_ref, kn_ref):
     head_dim = q_ref.shape[0]
-    h_rows = layer_norm(x_ref[...].astype(F32), gain_ref[...], bias_ref[...])[0].astype(BF16)
+    x_norm = layer_norm(x_ref[...].astype(F32), 1.0, 0.0)[1]
+    h_rows = (x_norm * gain_ref[...] + bias_ref[...]).astype(BF16)
     h_ref[...] = h_rows
+    m_ref[...] = (x_norm * gain2_ref[...] + bias2_ref[...]).astype(BF16)
     qkv = dot_nt(w_ref[...], h_rows) + b_ref[...]
     cos_t, sin_t = cos_ref[...], sin_ref[...]
     q_ref[...] = rotate_t(qkv[:head_dim], cos_t, sin_t).astype(BF16)
@@ -65,24 +68,67 @@
     v_ref[...] = qkv[2 * head_dim:].astype(BF16)
 
 
-def pre_call(x_all, gain, bias, w_head, b_head, cos_t, sin_t, rows):
+def pre_call(x_all, gains, w_head, b_head, cos_t, sin_t, rows):
     seq, width = x_all.shape
     head_dim = w_head.shape[0] // 3
     half = cos_t.shape[0]
     whole = lambda shape: pl.BlockSpec(shape, lambda i: (0,) * len(shape))
     cols = lambda n: pl.BlockSpec((n, rows), lambda i: (0, i))
+    wide = pl.BlockSpec((rows, width), lambda i: (i, 0))
     return pl.pallas_call(
         pre_kernel,
         grid=(seq // rows,),
-        in_specs=[pl.BlockSpec((rows, width), lambda i: (i, 0)), whole((1, width)), whole((1, width)),
-                  whole(w_head.shape), whole(b_head.shape), cols(half), cols(half)],
-        out_specs=[pl.BlockSpec((rows, width), lambda i: (i, 0)), cols(head_dim), cols(head_dim), cols(head_dim),
-                   pl.BlockSpec((rows, head_dim), lambda i: (i, 0))],
-        out_shape=[jax.ShapeDtypeStruct((seq, width), BF16)] + [jax.ShapeDtypeStruct((head_dim, seq), BF16)] * 3
+        in_specs=[wide] + [whole((1, width))] * 4 + [whole(w_head.shape), whole(b_head.shape), cols(half), cols(half)],
+        out_specs=[wide, wide, cols(head_dim), cols(head_dim), cols(head_dim), pl.BlockSpec((rows, head_dim), lambda i: (i, 0))],
+        out_shape=[jax.ShapeDtypeStruct((seq, width), BF16)] * 2 + [jax.ShapeDtypeStruct((head_dim, seq), BF16)] * 3
         + [jax.ShapeDtypeStruct((seq, head_dim), BF16)],
-        cost_estimate=pl.CostEstimate(flops=2 * seq * width * w_head.shape[0] * 3, bytes_accessed=seq * width * 4, transcendentals=0),
+        cost_estimate=pl.CostEstimate(flops=2 * seq * width * w_head.shape[0] * 3, bytes_accessed=seq * width * 6, transcendentals=0),
         name="pre",
-    )(x_all, gain, bias, w_head, b_head, cos_t, sin_t)
+    )(x_all, *gains, w_head, b_head, cos_t, sin_t)
+
+
+def mlp_kernel(core_ref, m_ref, dy_ref, wu_ref, bu_ref, wd_ref, ctx_ref, dwu_ref, dwd_ref, dbu_ref, dwo_ref, *, par):
+    step = pl.program_id(0)
+    rows = ctx_ref.shape[2]
+
+    @pl.when(step == 0)
+    def _():
+        for ref in (dwu_ref, dwd_ref, dbu_ref, dwo_ref):
+            ref[...] = jnp.zeros_like(ref)
+
+    m_rows, dy_rows = m_ref[...], dy_ref[...]
+    up = dot_nt(wu_ref[...], m_rows) + bu_ref[...]
+    cdf = 0.5 + 0.5 * lax.erf(up * (0.5 ** 0.5))
+    gelu = (up * cdf).astype(BF16)
+    d_gelu = dot_nt(wd_ref[...], dy_rows)
+    d_up = d_gelu * (cdf + up * (jnp.exp(up * up * -0.5) * (2 * math.pi) ** -0.5))
+    dwu_ref[...] += dot(d_up.astype(BF16), m_rows)
+    dwd_ref[...] += dot(gelu, dy_rows)
+    lanes = dbu_ref.shape[1]
+    dbu_ref[...] += sum(d_up[:, i * lanes:(i + 1) * lanes] for i in range(d_up.shape[1] // lanes))
+    own = pl.ds(pl.multiple_of(core_ref[0] * rows, rows), rows)
+    dwo_ref[...] += dot(ctx_ref[0], dy_ref[own, :])
+
+
+def mlp_call(core, m_all, dy_all, wu, bu, wd, ctx_t, par):
+    seq, width = m_all.shape
+    steps, head_dim, rows = ctx_t.shape
+    span = seq // steps
+    part = wu.shape[0]
+    whole = lambda shape: pl.BlockSpec(shape, lambda i, core_ref: (0,) * len(shape))
+    wide = pl.BlockSpec((span, width), lambda i, core_ref: (i, 0))
+    return pl.pallas_call(
+        functools.partial(mlp_kernel, par=par),
+        grid_spec=pltpu.PrefetchScalarGridSpec(
+            num_scalar_prefetch=1, grid=(steps,),
+            in_specs=[wide, wide, whole((part, width)), whole((part, 1)), whole((part, width)),
+                      pl.BlockSpec((1, head_dim, rows), lambda i, core_ref: (i, 0, 0))],
+            out_specs=[whole((part, width)), whole((part, width)), whole((part, 128)), whole((head_dim, width))]),
+        out_shape=[jax.ShapeDtypeStruct((part, width), F32), jax.ShapeDtypeStruct((part, width), F32),
+                   jax.ShapeDtypeStruct((part, 128), F32), jax.ShapeDtypeStruct((head_dim, width), F32)],
+        cost_estimate=pl.CostEstimate(flops=16 * seq * width * part, bytes_accessed=seq * width * 4, transcendentals=2 * seq * part),
+        name="mlp_grad",
+    )(core, m_all, dy_all, wu, bu, wd, ctx_t)
 
 
 def fwd_kernel(core_ref, kn_ref, q_ref, v_ref, ctx_ref, norm_ref, lse_ref, max_s, sum_s, acc_s, *, par, sub, scale2):
@@ -154,8 +200,8 @@
     )(core, k_nat, q_t, v_t)
 
 
-def bwd_kernel(core_ref, k_ref, kn_ref, v_ref, q_ref, dy_ref, w_ref, ctx_ref, norm_ref, lse_ref,
-               dq_ref, dk_ref, dv_ref, dw_ref, dq_s, *, par, sub, scale, scale2):
+def bwd_kernel(core_ref, k_ref, kn_ref, v_ref, q_ref, dy_ref, w_ref, norm_ref, lse_ref,
+               dq_ref, dkv_ref, dq_s, *, par, sub, scale, scale2):
     step = pl.program_id(0)
     core = core_ref[0]
     rows = q_ref.shape[1]
@@ -163,9 +209,7 @@
 
     @pl.when(step == 0)
     def _():
-        dk_ref[...] = jnp.zeros_like(dk_ref)
-        dv_ref[...] = jnp.zeros_like(dv_ref)
-        dw_ref[...] = jnp.zeros_like(dw_ref)
+        dkv_ref[...] = jnp.zeros_like(dkv_ref)
 
     q_t = q_ref[...]
     q_n = q_t.T
@@ -174,7 +218,6 @@
     delta = jnp.sum(d_ctx * norm_ref[0], axis=0, keepdims=True)
     do_t = d_ctx.astype(BF16)
     do_n = do_t.T
-    dw_ref[...] += dot(ctx_ref[0], dy_rows)
     lanes = 128
     spread = lambda row: jnp.concatenate([jnp.broadcast_to(row, (lanes, rows)).T] * (sub // lanes), axis=1)
     lse_c = spread(lse_ref[0])
@@ -194,8 +237,9 @@
                     q_pos = core * rows + lax.broadcasted_iota(jnp.int32, probs.shape, 0)
                     probs = jnp.where(key_pos <= q_pos, probs, 0.0)
                 d_scores = (probs * (dot(do_n, v_t) - delta_c)).astype(BF16)
-                dv_ref[i * par + b, :, cols] += dot(do_t, probs.astype(BF16))
-                dk_ref[i * par + b, :, cols] += dot(q_t, d_scores)
+                rel = lax.rem(core + b, par)
+                dkv_ref[rel, 1, i, :, cols] += dot(do_t, probs.astype(BF16))
+                dkv_ref[rel, 0, i, :, cols] += dot(q_t, d_scores)
                 dq_s[...] += dot(d_scores, kn_ref[pl.ds(start, sub), :])
 
     chunk(step, True)
@@ -207,7 +251,7 @@
     dq_ref[0] = dq_s[...].T * scale
 
 
-def bwd_call(core, k_t, k_nat, v_t, q_t, dy_all, w_head, ctx_t, norm_t, lse, rows, par, scale, scale2):
+def bwd_call(core, k_t, k_nat, v_t, q_t, dy_all, w_head, norm_t, lse, rows, par, scale, scale2):
     seq, head_dim = k_nat.shape
     width = dy_all.shape[-1]
     steps = seq // (rows * par)
@@ -221,14 +265,84 @@
             in_specs=[whole((head_dim, seq)), whole((seq, head_dim)), whole((head_dim, seq)),
                       pl.BlockSpec((head_dim, rows), lambda i, core_ref: (0, i * par + core_ref[0])),
                       pl.BlockSpec((1, rows, width), lambda i, core_ref: (i * par + core_ref[0], 0, 0)),
-                      whole((head_dim, width)), tile(head_dim), tile(head_dim), tile(1)],
-            out_specs=[tile(head_dim), whole((steps * par, head_dim, rows)), whole((steps * par, head_dim, rows)), whole((head_dim, width))],
+                      whole((head_dim, width)), tile(head_dim), tile(1)],
+            out_specs=[tile(head_dim), whole((par, 2, steps, head_dim, rows))],
             scratch_shapes=[pltpu.VMEM((rows, head_dim), F32)]),
-        out_shape=[jax.ShapeDtypeStruct((steps, head_dim, rows), F32), jax.ShapeDtypeStruct((steps * par, head_dim, rows), F32),
-                   jax.ShapeDtypeStruct((steps * par, head_dim, rows), F32), jax.ShapeDtypeStruct((head_dim, width), F32)],
+        out_shape=[jax.ShapeDtypeStruct((steps, head_dim, rows), F32), jax.ShapeDtypeStruct((par, 2, steps, head_dim, rows), F32)],
         cost_estimate=pl.CostEstimate(flops=64 * seq * seq * head_dim // par, bytes_accessed=seq * head_dim * 32, transcendentals=seq * seq // 4),
         name="attn_bwd",
-    )(core, k_t, k_nat, v_t, q_t, dy_all.reshape(-1, rows, width), w_head, ctx_t, norm_t, lse)
+    )(core, k_t, k_nat, v_t, q_t, dy_all.reshape(-1, rows, width), w_head, norm_t, lse)
+
+
+def post_kernel(core_ref, dq_ref, mine_ref, got_ref, cos_ref, sin_ref, h_ref, out_ref, dw_ref, db_ref, *, scale):
+    @pl.when(pl.program_id(0) == 0)
+    def _():
+        dw_ref[...] = jnp.zeros_like(dw_ref)
+        db_ref[...] = jnp.zeros_like(db_ref)
+
+    cos_t, sin_t = cos_ref[...], -sin_ref[...]
+    d_q = rotate_t(dq_ref[0], cos_t, sin_t)
+    d_k = rotate_t((mine_ref[0, 0, 0] + got_ref[0, 0]) * scale, cos_t, sin_t)
+    d_v = mine_ref[0, 1, 0] + got_ref[1, 0]
+    d_qkv = jnp.concatenate([d_q, d_k, d_v], axis=0)
+    lanes = db_ref.shape[1]
+    db_ref[...] += sum(d_qkv[:, i * lanes:(i + 1) * lanes] for i in range(d_qkv.shape[1] // lanes))
+    d_qkv = d_qkv.astype(BF16)
+    out_ref[0] = d_qkv
+    dw_ref[...] += dot(d_qkv, h_ref[...])
+
+
+def post_call(core, d_q, dkv, got, cos_t, sin_t, h_all, par, scale):
+    steps, head_dim, rows = d_q.shape
+    width = h_all.shape[1]
+    half = cos_t.shape[0]
+    own_cols = pl.BlockSpec((half, rows), lambda i, core_ref: (0, i * par + core_ref[0]))
+    whole = lambda shape: pl.BlockSpec(shape, lambda i, core_ref: (0,) * len(shape))
+    return pl.pallas_call(
+        functools.partial(post_kernel, scale=scale),
+        grid_spec=pltpu.PrefetchScalarGridSpec(
+            num_scalar_prefetch=1, grid=(steps,),
+            in_specs=[pl.BlockSpec((1, head_dim, rows), lambda i, core_ref: (i, 0, 0)),
+                      pl.BlockSpec((1, 2, 1, head_dim, rows), lambda i, core_ref: (0, 0, i, 0, 0)),
+                      pl.BlockSpec((2, 1, head_dim, rows), lambda i, core_ref: (0, i, 0, 0)),
+                      own_cols, own_cols, pl.BlockSpec((rows, width), lambda i, core_ref: (i * par + core_ref[0], 0))],
+            out_specs=[pl.BlockSpec((1, 3 * head_dim, rows), lambda i, core_ref: (i, 0, 0)), whole((3 * head_dim, width)), whole((3 * head_dim, 128))]),
+        out_shape=[jax.ShapeDtypeStruct((steps, 3 * head_dim, rows), BF16), jax.ShapeDtypeStruct((3 * head_dim, width), F32),
+                   jax.ShapeDtypeStruct((3 * head_dim, 128), F32)],
+        cost_estimate=pl.CostEstimate(flops=6 * steps * head_dim * rows * width, bytes_accessed=steps * rows * width * 4, transcendentals=0),
+        name="post",
+    )(core, d_q, dkv, got, cos_t, sin_t, h_all)
+
+
+def share_kernel(x_ref, o_ref, held, send_sem, recv_sem, *, size):
+    me = lax.axis_index('cp')
+    barrier = pltpu.get_barrier_semaphore()
+    for i in range(1, size):
+        pl.semaphore_signal(barrier, inc=1, device_id={'cp': lax.rem(me + i, size)}, device_id_type=pl.DeviceIdType.MESH)
+    pl.semaphore_wait(barrier, size - 1)
+    copies = []
+    for i in range(1, size):
+        copy = pltpu.make_async_remote_copy(src_ref=x_ref, dst_ref=held.at[i - 1], send_sem=send_sem.at[i - 1], recv_sem=recv_sem.at[i - 1],
+                                            device_id={'cp': lax.rem(me + i, size)}, device_id_type=pl.DeviceIdType.MESH)
+        copy.start()
+        copies.append(copy)
+    o_ref[0] = x_ref[...]
+    for i in range(1, size):
+        copies[i - 1].wait()
+        o_ref[i] = held[i - 1]
+
+
+def share_call(vec, size):
+    rows, lanes = vec.shape
+    spec = pl.BlockSpec(memory_space=pltpu.VMEM)
+    return pl.pallas_call(
+        functools.partial(share_kernel, size=size),
+        in_specs=[spec], out_specs=spec,
+        out_shape=jax.ShapeDtypeStruct((size, rows, lanes), F32),
+        scratch_shapes=[pltpu.VMEM((size - 1, rows, lanes), F32), pltpu.SemaphoreType.DMA((size - 1,)), pltpu.SemaphoreType.DMA((size - 1,))],
+        compiler_params=pltpu.CompilerParams(collective_id=0, has_side_effects=True),
+        name="share",
+    )(vec)
 
 
 def exact_gelu(pre_act):
@@ -263,57 +377,72 @@
         h_mlp = h_mlp.astype(BF16)
         up_proj = dot(h_mlp, w_up) + b_up.astype(F32)
         gelu_out, gelu_back = jax.vjp(exact_gelu, up_proj)
-        gelu_bf = gelu_out.astype(BF16)
-        mlp_proj = dot(gelu_bf, w_down) + b_down.astype(F32)
+        mlp_proj = dot(gelu_out.astype(BF16), w_down) + b_down.astype(F32)
         dy_sum = jnp.sum(dy_own, axis=0)
-        d_w_down = dot(gelu_bf.T, dy_bf)
         d_up = gelu_back(dot_nt(dy_bf, w_down))[0]
-        d_b_up = jnp.sum(d_up, axis=0)
-        d_up_bf = d_up.astype(BF16)
-        d_w_up = dot(h_mlp.T, d_up_bf)
-        d_h_mlp = dot_nt(d_up_bf, w_up)
+        d_h_mlp = dot_nt(d_up.astype(BF16), w_up)
         dx_mlp, d_ln2_gain, d_ln2_bias = norm_backward(d_h_mlp, x_norm, inv_std, ln2_gain)
-        early = lax.psum((d_w_up, d_w_down, d_b_up, dy_sum, d_ln2_gain, d_ln2_bias), 'cp')
-
+        y_part = x_rows + mlp_proj + b_out.astype(F32)
+        dx_part = dy_own + dx_mlp
+
+        ff = w_up.shape[1]
+        part = ff // cp_size
         cos_t, sin_t = rope_tables(jnp.arange(seq), head_dim)
         w_head = lax.dynamic_index_in_dim(w_qkv, head, axis=1, keepdims=False).reshape(width, 3 * head_dim).T
         b_head = lax.dynamic_index_in_dim(b_qkv, head, axis=0, keepdims=False).reshape(3 * head_dim, 1).astype(F32)
         wo_head = lax.dynamic_slice_in_dim(w_out, head * head_dim, head_dim, axis=0)
-        h_all, q_t, k_t, v_t, k_nat = pre_call(x_all, ln1_gain[None], ln1_bias[None], w_head, b_head, cos_t, sin_t, rows)
+        wu_part = lax.dynamic_slice_in_dim(w_up, me * part, part, axis=1).T
+        bu_part = lax.dynamic_slice_in_dim(b_up, me * part, part, axis=0).astype(F32)[:, None]
+        wd_part = lax.dynamic_slice_in_dim(w_down, me * part, part, axis=0)
+        gains = (ln1_gain[None], ln1_bias[None], ln2_gain[None], ln2_bias[None])
+        x_all, y_part, dx_part = lax.optimization_barrier((x_all, y_part, dx_part))
+        h_all, m_all, q_t, k_t, v_t, k_nat = pre_call(x_all, gains, w_head, b_head, cos_t, sin_t, rows * par)
         ctx_t, norm_t, lse = fwd_call(core_arr, k_nat, q_t, v_t, rows, par, scale2)
-
-        ctx_mine = lax.all_to_all(ctx_t, 'cp', 0, 0, axis_index_groups=same_core, tiled=True).reshape(width, rows)
-        attn_proj = dot(ctx_mine.T, w_out) + b_out.astype(F32)
-        y_rows = (x_rows + attn_proj + mlp_proj).astype(BF16)
-
-        d_q, dk_part, dv_part, dwo_part = bwd_call(core_arr, k_t, k_nat, v_t, q_t, dy_all, wo_head, ctx_t, norm_t, lse, rows, par, scale, scale2)
-        dkv_part = jnp.stack([dk_part, dv_part]).reshape(2, heads, par, head_dim, rows)
-        other = lax.dynamic_index_in_dim(dkv_part, par - 1 - core, axis=2, keepdims=False)
-        mine = lax.dynamic_index_in_dim(dkv_part, core, axis=2, keepdims=False)
+        ctx_parts, w_parts = [], []
+        w_heads = w_out.reshape(heads, head_dim, width)
+        for d in range(heads):
+            piece = lax.dynamic_index_in_dim(ctx_t, lax.rem(head + d, heads), keepdims=False)
+            away = [(z * par + c, (z + d) % heads * par + c) for z in range(heads) for c in range(par)]
+            ctx_parts.append(piece if d == 0 else lax.ppermute(piece, 'cp', away))
+            w_parts.append(lax.dynamic_index_in_dim(w_heads, lax.rem(head - d + heads, heads), keepdims=False))
+        d_wu, d_wd, d_bu, d_wo = mlp_call(core_arr, m_all, dy_all, wu_part, bu_part, wd_part, ctx_t, par)
+        d_w_up_t = lax.all_gather(d_wu, 'cp', tiled=True)
+        d_w_down = lax.all_gather(d_wd, 'cp', tiled=True)
+        d_w_out = lax.all_gather(d_wo, 'cp')
+        lse, d_wu = lax.optimization_barrier((lse, d_wu))
+        d_q, dkv = bwd_call(core_arr, k_t, k_nat, v_t, q_t, dy_all, wo_head, norm_t, lse, rows, par, scale, scale2)
+        d_w_up = d_w_up_t.T
+        d_w_out = jnp.sum(d_w_out.reshape(heads, par, head_dim, width), axis=1).reshape(width, width)
+        ctx_mine, w_mine = jnp.concatenate(ctx_parts, axis=0), jnp.concatenate(w_parts, axis=0)
+        attn_proj = lax.dot_general(ctx_mine, w_mine, (((0,), (0,)), ((), ())), preferred_element_type=F32)
+        y_rows = (y_part + attn_proj).astype(BF16)
+
         swap = [(z * par + c, z * par + par - 1 - c) for z in range(heads) for c in range(par)]
-        d_k, d_v = mine + lax.ppermute(other, 'cp', swap)
-        d_k = d_k * scale
-        own_cos = lax.dynamic_index_in_dim(cos_t.reshape(-1, heads, par, rows), core, axis=2, keepdims=False)
-        own_sin = lax.dynamic_index_in_dim(sin_t.reshape(-1, heads, par, rows), core, axis=2, keepdims=False)
-        unrotate = jax.vmap(rotate_t, in_axes=(0, 1, 1))
-        d_qkv = jnp.concatenate([unrotate(d_q, own_cos, -own_sin), unrotate(d_k, own_cos, -own_sin), d_v], axis=1)
-        d_b_head = jnp.sum(d_qkv, axis=(0, 2))
-        d_qkv = d_qkv.astype(BF16)
+        got = lax.ppermute(dkv[1], 'cp', swap)
+        d_qkv, d_w_head, d_b_head = post_call(core_arr, d_q, dkv, got, cos_t, sin_t, h_all, par, scale)
         d_qkv_mine = lax.all_to_all(d_qkv, 'cp', 0, 0, axis_index_groups=same_core, tiled=True).reshape(heads * 3 * head_dim, rows)
+        halves = d_w_head.reshape(par, -1, width)
+        d_w_half = lax.dynamic_index_in_dim(halves, core, keepdims=False) + lax.ppermute(lax.dynamic_index_in_dim(halves, par - 1 - core, keepdims=False), 'cp', swap)
+        d_w_qkv_t = lax.all_gather(d_w_half, 'cp', tiled=True)
+        d_w_qkv = d_w_qkv_t.T.reshape(w_qkv.shape)
         d_h = lax.dot_general(d_qkv_mine, w_qkv.reshape(width, -1), (((0,), (1,)), ((), ())), preferred_element_type=F32)
-        x_norm1 = x_norm
-        dx_attn, d_ln1_gain, d_ln1_bias = norm_backward(d_h, x_norm1, inv_std, ln1_gain)
-        dx_rows = dy_own + dx_attn + dx_mlp
-
-        h_own = lax.dynamic_index_in_dim(h_all.reshape(heads, par, rows, width), core, axis=1, keepdims=False)
-        d_w_head = jnp.einsum('ztd,zet->de', h_own, d_qkv, preferred_element_type=F32)
-        d_w_full = jnp.zeros((width, heads, 3 * head_dim), F32)
-        d_w_full = lax.dynamic_update_slice(d_w_full, d_w_head[:, None], (0, head, 0)).reshape(w_qkv.shape)
-        d_b_full = lax.dynamic_update_slice(jnp.zeros((heads, 3 * head_dim), F32), d_b_head[None], (head, 0)).reshape(b_qkv.shape)
-        d_wo_full = lax.dynamic_update_slice(jnp.zeros((width, width), F32), dwo_part, (head * head_dim, 0))
-        late, early = lax.optimization_barrier(((d_w_full, d_b_full, d_wo_full, d_ln1_gain, d_ln1_bias), early))
-        d_w_up, d_w_down, d_b_up, dy_sum, d_ln2_gain, d_ln2_bias = early
-        d_w_qkv, d_b_qkv, d_w_out, d_ln1_gain, d_ln1_bias = lax.psum(late, 'cp')
+        dx_attn, d_ln1_gain, d_ln1_bias = norm_backward(d_h, x_norm, inv_std, ln1_gain)
+        dx_rows = dx_part + dx_attn
+
+        small = [d_ln1_gain, d_ln1_bias, d_ln2_gain, d_ln2_bias, dy_sum, jnp.sum(d_b_head, axis=1), jnp.sum(d_bu, axis=1)]
+        sizes = [v.shape[0] for v in small]
+        total = sum(sizes)
+        padded = -(-total // 1024) * 1024
+        vec = jnp.concatenate(small + [jnp.zeros((padded - total,), F32)]).reshape(-1, 128)
+        shared = share_call(vec, cp_size).reshape(cp_size, padded)
+        ends = [sum(sizes[:i]) for i in range(len(sizes) + 1)]
+        sums = jnp.sum(shared[:, :ends[5]], axis=0)
+        d_ln1_gain, d_ln1_bias, d_ln2_gain, d_ln2_bias, dy_sum = (sums[ends[i]:ends[i + 1]] for i in range(5))
+        origin = lax.rem(me - jnp.arange(cp_size) + cp_size, cp_size)
+        place = (origin[None, :] == jnp.arange(cp_size)[:, None])[:, :, None]
+        ordered = jnp.sum(jnp.where(place, shared[None, :, ends[5]:ends[7]], 0.0), axis=1)
+        d_b_qkv = jnp.sum(ordered[:, :sizes[5]].reshape(heads, par, -1), axis=1).reshape(b_qkv.shape)
+        d_b_up = ordered[:, sizes[5]:].reshape(ff)
         return (y_rows[None], dx_rows[None], d_ln1_gain, d_ln1_bias, d_ln2_gain, d_ln2_bias, d_w_qkv, d_b_qkv, d_w_out, dy_sum, d_w_up, d_b_up, d_w_down, dy_sum)
 
     return jax.shard_map(local_layer, mesh=mesh, in_specs=in_specs, out_specs=out_specs, check_vma=False)

time: 513 us -> 346 us (0.67)
  waiting for transfers between devices: 177 us -> 70.8 us
  blocking collectives: 88.8 us -> 0 us
  Pallas kernels: 131 us -> 164 us
  matrix products: 42.3 us -> 30.8 us
  other arithmetic: 25.6 us -> 17.9 us
  local copies, waits for them, and re-layouts: 21.9 us -> 29.3 us
    psum x2 -> x0, waiting for transfers between devices: 95.8 us -> none  [the longest x1 48.8 us: local_layer(): d_w_qkv, d_b_qkv, d_w_out, d_ln1_gain, d_ln1_bias = lax.psum(late, 'cp')]
    psum x2 -> x0, blocking collectives: 88.8 us -> none  [the longest x1 45.5 us: local_layer(): d_w_qkv, d_b_qkv, d_w_out, d_ln1_gain, d_ln1_bias = lax.psum(late, 'cp')]
    ppermute x1 -> x9, waiting for transfers between devices: 0.01 us -> 53.6 us  [the longest x7 48.2 us: local_layer(): ctx_parts.append(piece if d == 0 else lax.ppermute(piece, 'cp', away))]
    all_to_all x1, waiting for transfers between devices: 35.3 us -> 0.01 us  [local_layer(): lax.all_to_all(d_qkv, 'cp', 0, 0, axis_index_groups=same_core, tiled=True)]
    pallas_call x1 -> x4, Pallas kernels: 17.3 us -> 50.8 us  [the longest x1 15.3 us: pre_call(): pl.pallas_call(pre_kernel, grid=(seq // rows,), in_specs=[wide] + [whole(...]
    all_gather x1, waiting for transfers between devices: 31.4 us -> 15.7 us  [local_layer(): x_all = lax.all_gather(x_own, 'cp', tiled=True)]
    all_to_all x1 -> x0, waiting for transfers between devices: 13.1 us -> none  [local_layer(): lax.all_to_all(ctx_t, 'cp', 0, 0, axis_index_groups=same_core, tiled=True)]
    ppermute x1 -> x9, starting transfers between devices: 0.27 us -> 11 us  [the longest x7 10.4 us: local_layer(): ctx_parts.append(piece if d == 0 else lax.ppermute(piece, 'cp', away))]
  transfers between devices with their start and end apart: 7 -> 16, of which waited for: 5 -> 7; matrix products, arithmetic and copies ran while one was open for 15% -> 20% of each run, Pallas kernels for 11% -> 44%
where the time goes in v2:
time: 346 us; the launch traced here: 344 us
  Pallas kernels  164 us (47%)
  waiting for transfers between devices  70.8 us (20%)
  matrix products  30.8 us (9%)
  local copies, waits for them, and re-layouts  29.3 us (8%)
  other arithmetic  17.9 us (5%)
  starting transfers between devices  16.2 us (5%)
  between operations  14.8 us (4%)
    pallas_call x1, Pallas kernels, bwd_call(): pl.pallas_call(functools.partial(bwd_kernel, par=par, sub=sub, scale=scal...  72.7 us
    ppermute x7, waiting for transfers between devices, local_layer(): ctx_parts.append(piece if d == 0 else lax.ppermute(piece, 'cp', away))  48.2 us
    pallas_call x1, Pallas kernels, fwd_call(): pl.pallas_call(functools.partial(fwd_kernel, par=par, sub=sub, scale2=sca...  40.8 us
    dot_general x2, matrix products, dot(): return jnp.dot(a, b, preferred_element_type=F32)  17.3 us
    unnamed x71, local copies, waits for them, and re-layouts  17 us
    all_gather x1, waiting for transfers between devices, local_layer(): x_all = lax.all_gather(x_own, 'cp', tiled=True)  15.7 us
    pallas_call x1, Pallas kernels, pre_call(): pl.pallas_call(pre_kernel, grid=(seq // rows,), in_specs=[wide] + [whole(...  15.3 us
    pallas_call x1, Pallas kernels, mlp_call(): pl.pallas_call(functools.partial(mlp_kernel, par=par), grid_spec=pltpu.Pr...  14.1 us
  transfers between devices with their start and end apart: 16, of which 7 were waited for; matrix products, arithmetic and copies ran while one was open for 20% of the time, Pallas kernels for 44%

profile of v2, /device:TPU:21, one launch (start us, length us, event | category | flops | bytes accessed | tf_op | source)
XLA Modules:
  0.0 344.3 jit_solution(9269942754644156655)
XLA Ops:
  7.3 0.7 all-gather.17.cloned.1.call-update
  8.1 2.7 fusion.52
  11.0 0.7 convert_element_type.48
  13.0 0.7 fusion.46
  13.7 0.8 reshape.185.b_ref
  14.5 0.8 copy.43
  15.3 0.8 bitcast_convert_fusion.1
  16.1 0.7 copy.38.bu_ref
  16.8 1.6 constant_dynamic-slice_fusion.wd_ref
  18.4 1.6 constant_dynamic-slice_fusion.4
  20.5 11.4 %fusion = (f32[512,2048]{1,0:T(8,128)}, f32[512,2048]{1,0:T(8,128)}) fusion(f32[2048]{0:T(1024)S(1)} %convert_element_type.48, bf16[512,2048]{1,0:T(8,128)(2,1)S(1)} %copy-done, bf16[1,512,512]{2,1,0:T(8,128)(2,1)S(1)} %copy-done.2, f32[512]{0:T(512)S(1)} %copy-done.24, f32[512]{0:T(512)S(1)} %copy-done.20, f32[512]{0:T(512)S(1)} %add_rsqrt_fusion, ...), kind=kOutput, calls=%fused_computation.1 | convolution fusion | flops 1141374976 | bytes 11026432 | tf_op jit(solution)/shard_map/dot_general | solution.py:21
  32.0 8.9 %fusion.37 = (f32[512]{0:T(512)}, f32[512]{0:T(512)S(1)}, f32[512]{0:T(512)S(1)}, f32[512]{0:T(512)}, f32[512,512]{1,0:T(8,128)}) fusion(bf16[1,512,512]{2,1,0:T(8,128)(2,1)S(1)} %copy-done.2, f32[512]{0:T(512)S(1)} %add_rsqrt_fusion, f32[512]{0:T(512)S(1)} %broadcast_multiply_fusion.4, f32[512]{0:T(512)S(1)} %copy-done.20, ...), kind=kOutput, calls=%fused_computation.52 | convolution fusion | flops 2165831680 | bytes 14702592 | tf_op jit(solution)/shard_map/dot_general | solution.py:25
  40.9 3.1 fusion.30
  44.0 5.9 %fusion.13 = f32[512,512]{1,0:T(8,128)} fusion(bf16[2048,512]{1,0:T(8,128)(2,1)S(1)} %copy-done.7, f32[512,2048]{1,0:T(8,128)} %get-tuple-element.124, f32[512,2048]{1,0:T(8,128)} %get-tuple-element.125, f32[2048]{0:T(1024)S(1)} %convert_element_type.48, bf16[1,512,512]{2,1,0:T(8,128)(2,1)S(1)} %copy-done.2, f32[512]{0:T(512)S(1)} %convert_element_type.51, ...), kind=kOutput, calls=%fused_computation.28 | convolution fusion | flops 1078984704 | bytes 12070912 | tf_op jit(solution)/shard_map/dot_general | solution.py:21
  49.9 1.8 multiply_sine_fusion
  51.7 15.7 %all-gather.17.cloned.1.call-done = bf16[1,8192,512]{2,1,0:T(8,128)(2,1)} async-done(((bf16[1,512,512]{2,1,0:T(8,128)(2,1)}), bf16[1,8192,512]{2,1,0:T(8,128)(2,1)}) %all-gather.17.cloned.1.call-update) | async-done | bytes 8388624 | tf_op jit(solution)/shard_map/all_gather | solution.py:372
  67.3 15.3 %pre.1 = (bf16[8192,512]{1,0:T(8,128)(2,1)}, bf16[8192,512]{1,0:T(8,128)(2,1)}, bf16[64,8192]{1,0:T(8,128)(2,1)}, bf16[64,8192]{1,0:T(8,128)(2,1)}, bf16[64,8192]{1,0:T(8,128)(2,1)}, /*index=5*/bf16[8192,64]{1,0:T(8,128)(2,1)}) custom-call(bf16[8192,512]{1,0:T(8,128)(2,1)} %bitcast.166, f32[1,512]{1,0:T(1,128)} %bitcast.164, f32[1,512]{1,0:T(1,128)} %bitcast.168, ...), custom_call_target="tpu_custom_call" | custom-call | flops 4831838208 | bytes 25165824 | tf_op jit(solution)/shard_map/pre/pallas_call | solution.py:78
  82.7 40.8 %attn_fwd.1 = (bf16[8,64,512]{2,1,0:T(8,128)(2,1)}, f32[8,64,512]{2,1,0:T(8,128)}, f32[8,1,512]{2,1,0:T(1,128)}) custom-call(s32[1]{0:T(128)} %bitcast.3.core_ref, bf16[8192,64]{1,0:T(8,128)(2,1)} %get-tuple-element.38.kn_ref, bf16[64,8192]{1,0:T(8,128)(2,1)} %get-tuple-element.39.q_ref, bf16[64,8192]{1,0:T(8,128)(2,1)} %get-tuple-element.40.v_ref), custom_call_target="tpu_custom_call" | custom-call | flops 68719476736 | bytes 4194304 | tf_op jit(solution)/shard_map/attn_fwd/pallas_call | solution.py:188
  123.5 14.1 %mlp_grad.1 = (f32[128,512]{1,0:T(8,128)}, f32[128,512]{1,0:T(8,128)}, f32[128,128]{1,0:T(8,128)}, f32[64,512]{1,0:T(8,128)}) custom-call(s32[1]{0:T(128)} %bitcast.3.core_ref, bf16[8192,512]{1,0:T(8,128)(2,1)} %get-tuple-element.46.m_ref, bf16[8192,512]{1,0:T(8,128)(2,1)} %all-gather.9.cloned.1.call-done.dy_ref, bf16[128,512]{1,0:T(8,128)(2,1)} %bitcast.160, ...), custom_call_target="tpu_custom_call" | custom-call | flops 8589934592 | bytes 16777216 | tf_op jit(solution)/shard_map/mlp_grad/pallas_call | solution.py:120
  139.4 72.7 %attn_bwd.1 = (f32[8,64,512]{2,1,0:T(8,128)}, f32[2,2,8,64,512]{4,3,2,1,0:T(8,128)}) custom-call(s32[1]{0:T(128)} %bitcast.3.core_ref, bf16[64,8192]{1,0:T(8,128)(2,1)} %get-tuple-element.43.k_ref, bf16[8192,64]{1,0:T(8,128)(2,1)} %get-tuple-element.38.kn_ref, bf16[64,8192]{1,0:T(8,128)(2,1)} %get-tuple-element.40.v_ref, ...), custom_call_target="tpu_custom_call" | custom-call | flops 137438953472 | bytes 16777216 | tf_op jit(solution)/shard_map/attn_bwd/pallas_call | solution.py:261
  212.1 3.1 slice_bitcast_fusion
  215.5 4.1 %collective-permute-done.7.got_ref = f32[2,8,64,512]{3,2,1,0:T(8,128)S(1)} collective-permute-done((f32[2,8,64,512]{3,2,1,0:T(8,128)}, f32[2,8,64,512]{3,2,1,0:T(8,128)S(1)}, u32[]{:S(2)}, u32[]{:S(2)}) %collective-permute-start.7) | collective-permute-done | bytes 2097184 | tf_op jit(solution)/shard_map/ppermute | solution.py:421
  219.7 1.3 copy-done.8
  221.0 7.9 %post.1 = (bf16[8,192,512]{2,1,0:T(8,128)(2,1)}, f32[192,512]{1,0:T(8,128)}, f32[192,128]{1,0:T(8,128)}) custom-call(s32[1]{0:T(128)} %bitcast.3.core_ref, f32[8,64,512]{2,1,0:T(8,128)} %get-tuple-element.49.dq_ref, f32[2,2,8,64,512]{4,3,2,1,0:T(8,128)} %get-tuple-element.50.mine_ref, f32[2,8,64,512]{3,2,1,0:T(8,128)} %copy-done.8, ...), custom_call_target="tpu_custom_call" | custom-call | flops 805306368 | bytes 8388608 | tf_op jit(solution)/shard_map/post/pallas_call | solution.py:301
  228.9 1.1 dynamic-slice_bitcast_fusion
  230.4 1.3 collective-permute-done.8
  231.7 1.6 bitcast_add_fusion
  233.4 4.6 %all-to-all-start = ((bf16[8,192,512]{2,1,0:T(8,128)(2,1)}), bf16[8,192,512]{2,1,0:T(8,128)(2,1)}, u32[]{:S(2)}, u32[]{:S(2)}) async-start(bf16[8,192,512]{2,1,0:T(8,128)(2,1)} %get-tuple-element.52), calls=%async_computation | async-start | bytes 3145728 | tf_op jit(solution)/shard_map/all_to_all | solution.py:423
  238.4 0.7 dynamic-slice_bitcast_fusion.1
  239.1 1.1 collective-permute-start
  240.2 2.1 collective-permute-start.1
  242.3 2.4 collective-permute-start.2
  244.7 2.1 collective-permute-start.3
  246.7 2.4 collective-permute-start.4
  249.3 0.9 bitcast_dynamic-update-slice_fusion.8
  250.1 31.5 %collective-permute-done = bf16[64,512]{1,0:T(8,128)(2,1)S(1)} collective-permute-done((bf16[64,512]{1,0:T(8,128)(2,1)S(1)}, bf16[64,512]{1,0:T(8,128)(2,1)S(1)}, u32[]{:S(2)}, u32[]{:S(2)}) %collective-permute-start) | collective-permute-done | bytes 65568 | tf_op jit(solution)/shard_map/ppermute | solution.py:406
  281.9 5.7 %collective-permute-done.1 = bf16[64,512]{1,0:T(8,128)(2,1)S(1)} collective-permute-done((bf16[64,512]{1,0:T(8,128)(2,1)}, bf16[64,512]{1,0:T(8,128)(2,1)S(1)}, u32[]{:S(2)}, u32[]{:S(2)}) %collective-permute-start.1) | collective-permute-done | bytes 65568 | tf_op jit(solution)/shard_map/ppermute | solution.py:406
  287.6 2.5 collective-permute-done.2
  290.2 8.5 %collective-permute-done.3 = bf16[64,512]{1,0:T(8,128)(2,1)S(1)} collective-permute-done((bf16[64,512]{1,0:T(8,128)(2,1)S(1)}, bf16[64,512]{1,0:T(8,128)(2,1)S(1)}, u32[]{:S(2)}, u32[]{:S(2)}) %collective-permute-start.3) | collective-permute-done | bytes 65568 | tf_op jit(solution)/shard_map/ppermute | solution.py:406
  298.8 1.3 fusion.24
  300.2 2.9 reduce_sum.169
  303.2 3.3 fusion.36
  307.1 13.5 %share.1 = f32[16,24,128]{2,1,0:T(8,128)} custom-call(f32[24,128]{1,0:T(8,128)} %bitcast.161), custom_call_target="tpu_custom_call" | custom-call | tf_op jit(solution)/shard_map/share/pallas_call | solution.py:338
  320.6 1.0 copy.46
  323.8 1.4 fusion.35
  325.2 5.3 %copy.41 = f32[512,2048]{1,0:T(8,128)} copy(f32[512,2048]{0,1:T(8,128)} %bitcast.142) | data formatting | bytes 8388608
  331.1 4.3 %copy.65 = f32[512,8,3,64]{0,3,2,1:T(8,128)} copy(f32[512,8,3,64]{0,3,2,1:T(8,128)} %bitcast.143) | data formatting | bytes 6291456
  335.4 2.0 copy.66
  (118 shorter events, 8.8 us)
Async XLA Ops:
  7.2 7.3 %copy-start = (bf16[512,2048]{1,0:T(8,128)(2,1)S(1)}, bf16[512,2048]{1,0:T(8,128)(2,1)}, u32[]{:S(2)}) copy-start(bf16[512,2048]{1,0:T(8,128)(2,1)} %param.24) | copy-start | bytes 6291460
  7.2 12.8 %copy-start.2 = (bf16[1,512,512]{2,1,0:T(8,128)(2,1)S(1)}, bf16[1,512,512]{2,1,0:T(8,128)(2,1)}, u32[]{:S(2)}) copy-start(bf16[1,512,512]{2,1,0:T(8,128)(2,1)} %param.14) | copy-start | bytes 1572868
  7.2 13.3 %copy-start.24 = (f32[512]{0:T(512)S(1)}, f32[512]{0:T(512)}, u32[]{:S(2)}) copy-start(f32[512]{0:T(512)} %param.19) | copy-start | bytes 6148
  7.2 13.3 %copy-start.20 = (f32[512]{0:T(512)S(1)}, f32[512]{0:T(512)}, u32[]{:S(2)}) copy-start(f32[512]{0:T(512)} %param.18) | copy-start | bytes 6148
  7.2 60.1 %all-gather.17.cloned.1.call-start = ((), (), s32[]{:S(2)}) async-start(), calls=%async_computation.5 | async-start | bytes 8912896 | tf_op jit(solution)/shard_map/all_gather | solution.py:372
  8.0 115.5 %all-gather.9.cloned.1.call-start = ((), (), s32[]{:S(2)}) async-start(), calls=%async_computation.1 | async-start | bytes 8912896 | tf_op jit(solution)/shard_map/all_gather | solution.py:373
  10.9 289.3 %all-gather.19.cloned.1.call-start = ((), (), s32[]{:S(2)}) async-start(), calls=%async_computation.6 | async-start | bytes 2228224 | tf_op jit(solution)/shard_map/all_gather | solution.py:411
  20.2 20.7 %copy-start.14 = (f32[512]{0:T(512)}, f32[512]{0:T(512)S(1)}, u32[]{:S(2)}) copy-start(f32[512]{0:T(512)S(1)} %broadcast_multiply_fusion.4) | copy-start | bytes 6148
  20.5 20.4 %copy-start.16 = (f32[512]{0:T(512)}, f32[512]{0:T(512)S(1)}, u32[]{:S(2)}) copy-start(f32[512]{0:T(512)S(1)} %add_rsqrt_fusion) | copy-start | bytes 6148
  20.5 11.4 %copy-start.9 = (bf16[512,512]{1,0:T(8,128)(2,1)S(1)}, bf16[512,512]{1,0:T(8,128)(2,1)}, u32[]{:S(2)}) copy-start(bf16[512,512]{1,0:T(8,128)(2,1)} %get-tuple-element.109) | copy-start | bytes 1572868
  40.9 3.1 copy-start.7
  123.5 15.1 %copy-start.10 = (bf16[512,512]{1,0:T(8,128)(2,1)S(1)}, bf16[512,512]{1,0:T(8,128)(2,1)}, u32[]{:S(2)}) copy-start(bf16[512,512]{1,0:T(8,128)(2,1)} %param.22) | copy-start | bytes 1572868
  137.7 187.5 %all-gather.13.cloned.1.call-start = ((), (), s32[]{:S(2)}) async-start(), calls=%async_computation.3 | async-start | bytes 4456448 | tf_op jit(solution)/shard_map/all_gather | solution.py:409
  138.4 192.2 %all-gather.15.cloned.1.call-start = ((), (), s32[]{:S(2)}) async-start(), calls=%async_computation.4 | async-start | bytes 4456448 | tf_op jit(solution)/shard_map/all_gather | solution.py:410
  139.3 191.2 %all-gather.11.cloned.1.call-start = ((), (), s32[]{:S(2)}) async-start(), calls=%async_computation.2 | async-start | bytes 3342336 | tf_op jit(solution)/shard_map/all_gather | solution.py:426
  215.3 4.4 %collective-permute-start.7 = (f32[2,8,64,512]{3,2,1,0:T(8,128)}, f32[2,8,64,512]{3,2,1,0:T(8,128)S(1)}, u32[]{:S(2)}, u32[]{:S(2)}) collective-permute-start(f32[2,8,64,512]{3,2,1,0:T(8,128)} %slice_bitcast_fusion), channel_id=1, source_target_pairs={{0,1},{1,0},{2,3},{3,2},{4,5},{5,4},{6,7},{7,6},{8,9},{9,8},{10,11... | collective-permute-start | bytes 6291464 | tf_op jit(solution)/shard_map/ppermute | solution.py:421
  219.6 1.3 copy-start.8
  228.9 9.5 %copy-start.11 = (bf16[8,64,512]{2,1,0:T(8,128)(2,1)S(1)}, bf16[8,64,512]{2,1,0:T(8,128)(2,1)}, u32[]{:S(2)}) copy-start(bf16[8,64,512]{2,1,0:T(8,128)(2,1)} %get-tuple-element.41.ctx_ref) | copy-start | bytes 1572868
  228.9 20.3 %copy-start.13 = (f32[128,128]{1,0:T(8,128)S(1)}, f32[128,128]{1,0:T(8,128)}, u32[]{:S(2)}) copy-start(f32[128,128]{1,0:T(8,128)} %get-tuple-element.54) | copy-start | bytes 196612
  228.9 69.8 %copy-start.5 = (f32[512,512]{1,0:T(8,128)S(1)}, f32[512,512]{1,0:T(8,128)}, u32[]{:S(2)}) copy-start(f32[512,512]{1,0:T(8,128)} %fusion.13) | copy-start | bytes 3145732
  230.0 1.6 collective-permute-start.8
  233.4 66.7 %copy-start.12 = (f32[192,128]{1,0:T(8,128)S(1)}, f32[192,128]{1,0:T(8,128)}, u32[]{:S(2)}) copy-start(f32[192,128]{1,0:T(8,128)} %get-tuple-element.53) | copy-start | bytes 294916
  233.4 69.7 %all-to-all-start = ((bf16[8,192,512]{2,1,0:T(8,128)(2,1)}), bf16[8,192,512]{2,1,0:T(8,128)(2,1)}, u32[]{:S(2)}, u32[]{:S(2)}) async-start(bf16[8,192,512]{2,1,0:T(8,128)(2,1)} %get-tuple-element.52), calls=%async_computation | async-start | bytes 3145728 | tf_op jit(solution)/shard_map/all_to_all | solution.py:423
  238.2 64.9 %copy-start.3 = (bf16[1,512,512]{2,1,0:T(8,128)(2,1)S(1)}, bf16[1,512,512]{2,1,0:T(8,128)(2,1)}, u32[]{:S(2)}) copy-start(bf16[1,512,512]{2,1,0:T(8,128)(2,1)} %param.14) | copy-start | bytes 1572868
  238.3 64.9 %copy-start.15 = (f32[512]{0:T(512)S(1)}, f32[512]{0:T(512)}, u32[]{:S(2)}) copy-start(f32[512]{0:T(512)} %copy-done.14) | copy-start | bytes 6148
  238.3 64.9 %copy-start.17 = (f32[512]{0:T(512)S(1)}, f32[512]{0:T(512)}, u32[]{:S(2)}) copy-start(f32[512]{0:T(512)} %copy-done.16) | copy-start | bytes 6148
  238.3 64.9 %copy-start.21 = (f32[512]{0:T(512)S(1)}, f32[512]{0:T(512)}, u32[]{:S(2)}) copy-start(f32[512]{0:T(512)} %param.16) | copy-start | bytes 6148
  239.1 42.5 %collective-permute-start = (bf16[64,512]{1,0:T(8,128)(2,1)S(1)}, bf16[64,512]{1,0:T(8,128)(2,1)S(1)}, u32[]{:S(2)}, u32[]{:S(2)}) collective-permute-start(bf16[64,512]{1,0:T(8,128)(2,1)S(1)} %get-tuple-element.116), channel_id=1, source_target_pairs={{0,2},{1,3},{2,4},{3,5},{4,6},{5,7},{6,8},{7,9},{8,10},{9,11},{10,... | collective-permute-start | bytes 196616 | tf_op jit(solution)/shard_map/ppermute | solution.py:406
  240.2 47.4 %collective-permute-start.1 = (bf16[64,512]{1,0:T(8,128)(2,1)}, bf16[64,512]{1,0:T(8,128)(2,1)S(1)}, u32[]{:S(2)}, u32[]{:S(2)}) collective-permute-start(bf16[64,512]{1,0:T(8,128)(2,1)} %get-tuple-element.115), channel_id=1, source_target_pairs={{0,4},{1,5},{2,6},{3,7},{4,8},{5,9},{6,10},{7,11},{8,12},{9,13},{1... | collective-permute-start | bytes 196616 | tf_op jit(solution)/shard_map/ppermute | solution.py:406
  242.3 47.9 %collective-permute-start.2 = (bf16[64,512]{1,0:T(8,128)(2,1)S(1)}, bf16[64,512]{1,0:T(8,128)(2,1)S(1)}, u32[]{:S(2)}, u32[]{:S(2)}) collective-permute-start(bf16[64,512]{1,0:T(8,128)(2,1)S(1)} %get-tuple-element.114), channel_id=1, source_target_pairs={{0,6},{1,7},{2,8},{3,9},{4,10},{5,11},{6,12},{7,13},{8,14},{9,15},... | collective-permute-start | bytes 196616 | tf_op jit(solution)/shard_map/ppermute | solution.py:406
  244.7 54.0 %collective-permute-start.3 = (bf16[64,512]{1,0:T(8,128)(2,1)S(1)}, bf16[64,512]{1,0:T(8,128)(2,1)S(1)}, u32[]{:S(2)}, u32[]{:S(2)}) collective-permute-start(bf16[64,512]{1,0:T(8,128)(2,1)S(1)} %get-tuple-element.113), channel_id=1, source_target_pairs={{0,8},{1,9},{2,10},{3,11},{4,12},{5,13},{6,14},{7,15},{8,0},{9,1},... | collective-permute-start | bytes 196616 | tf_op jit(solution)/shard_map/ppermute | solution.py:406
  246.7 52.0 %collective-permute-start.4 = (bf16[64,512]{1,0:T(8,128)(2,1)S(1)}, bf16[64,512]{1,0:T(8,128)(2,1)S(1)}, u32[]{:S(2)}, u32[]{:S(2)}) collective-permute-start(bf16[64,512]{1,0:T(8,128)(2,1)S(1)} %get-tuple-element.112), channel_id=1, source_target_pairs={{0,10},{1,11},{2,12},{3,13},{4,14},{5,15},{6,0},{7,1},{8,2},{9,3},... | collective-permute-start | bytes 196616 | tf_op jit(solution)/shard_map/ppermute | solution.py:406
  281.6 17.1 %collective-permute-start.5 = (bf16[64,512]{1,0:T(8,128)(2,1)S(1)}, bf16[64,512]{1,0:T(8,128)(2,1)S(1)}, u32[]{:S(2)}, u32[]{:S(2)}) collective-permute-start(bf16[64,512]{1,0:T(8,128)(2,1)S(1)} %get-tuple-element.111), channel_id=1, source_target_pairs={{0,12},{1,13},{2,14},{3,15},{4,0},{5,1},{6,2},{7,3},{8,4},{9,5},{1... | collective-permute-start | bytes 196616 | tf_op jit(solution)/shard_map/ppermute | solution.py:406
  287.6 11.1 %collective-permute-start.6 = (bf16[64,512]{1,0:T(8,128)(2,1)S(1)}, bf16[64,512]{1,0:T(8,128)(2,1)S(1)}, u32[]{:S(2)}, u32[]{:S(2)}) collective-permute-start(bf16[64,512]{1,0:T(8,128)(2,1)S(1)} %get-tuple-element.110), channel_id=1, source_target_pairs={{0,14},{1,15},{2,0},{3,1},{4,2},{5,3},{6,4},{7,5},{8,6},{9,7},{10,... | collective-permute-start | bytes 196616 | tf_op jit(solution)/shard_map/ppermute | solution.py:406
  303.1 3.3 copy-start.18
  303.1 3.4 copy-start.22
  303.1 3.4 copy-start.23
  303.1 20.7 %copy-start.4 = (f32[512,512]{1,0:T(8,128)S(1)}, f32[512,512]{1,0:T(8,128)}, u32[]{:S(2)}) copy-start(f32[512,512]{1,0:T(8,128)} %fusion.30) | copy-start | bytes 3145732
  323.1 7.4 %copy-start.19 = (f32[512]{0:T(512)}, f32[512]{0:T(512)S(1)}, u32[]{:S(2)}) copy-start(f32[512]{0:T(512)S(1)} %get-tuple-element.181) | copy-start | bytes 6148
  330.5 4.9 %copy-start.6 = (f32[2048,512]{1,0:T(8,128)S(1)}, f32[2048,512]{1,0:T(8,128)}, u32[]{:S(2)}) copy-start(f32[2048,512]{1,0:T(8,128)} %all-gather.15.cloned.1.call-done) | copy-start | bytes 12582916
  331.1 6.3 %copy-start.1 = (bf16[512,2048]{1,0:T(8,128)(2,1)S(1)}, bf16[512,2048]{1,0:T(8,128)(2,1)}, u32[]{:S(2)}) copy-start(bf16[512,2048]{1,0:T(8,128)(2,1)} %param.24) | copy-start | bytes 6291460
Sparse Core Ops, SparseCore 0:
  9.7 57.5 all-gather.16
  69.0 51.1 all-gather.8
  137.8 34.8 all-gather.18
  174.2 37.2 all-gather.12
  213.0 54.2 all-gather.14
  269.4 43.5 all-gather.10
